TPU v7x, 32 devices: a 4x2x2 block of a 4x4x8 slice. The times are simulated.
32 devices in a mesh: dp: 4 (over y, z), ep: 8 (over x, core).
Axes of the slice: x: 4, y: 2, z: 2, core: 2. Of those that a mesh axis runs over, the one named last changes fastest.
The devices are a block of a 4x4x8 slice.
Arguments:
- tokens: bfloat16 [2048, 2048], P(('dp', 'ep')), parts along dimension 0
- slot_ids: int32 [2048, 4, 32], P(('dp', 'ep')), parts along dimension 0
- request_rows: int32 [32, 8, 128], P(('dp', 'ep')), parts along dimension 0
- gate_vals: float32 [2048, 4, 32], P(('dp', 'ep')), parts along dimension 0
- grad_out: bfloat16 [2048, 2048], P(('dp', 'ep')), parts along dimension 0
- table_up: bfloat16 [16384, 2048], P('ep')
- table_down: bfloat16 [16384, 2048], P('ep')
Outputs:
- output 1: bfloat16 [2048, 2048], P(('dp', 'ep')), parts along dimension 0
- output 2: bfloat16 [2048, 2048], P(('dp', 'ep')), parts along dimension 0
- output 3: bfloat16 [65536, 2048], P(('dp', 'ep')), parts along dimension 0
- output 4: bfloat16 [65536, 2048], P(('dp', 'ep')), parts along dimension 0
There are 4 independent parts. A program takes and returns all parts, laid end to end along the dimension named above; an argument that names none is the same for every part.
All inputs are finite; a program needn't handle non-finite values.
Results may differ from a plain program's by a relative error of at most 0.00871581.
Values are sent between devices in bfloat16 or wider.
A program may use at most 768 MiB of HBM per device.

v0:
```python
import math
import jax
import jax.numpy as jnp
from jax import lax
from jax.sharding import PartitionSpec as P


def gelu_pair(pre_act):
    normal_cdf = 0.5 * (1.0 + lax.erf(pre_act * (2.0 ** -0.5)))
    normal_pdf = jnp.exp(-0.5 * pre_act * pre_act) * ((2.0 * math.pi) ** -0.5)
    return pre_act * normal_cdf, normal_cdf + pre_act * normal_pdf


def local_layer(tokens, slot_flat, gate_flat, grad_out, up_table, down_table):
    tok_dev, width = tokens.shape
    sel_tok = slot_flat.shape[1]
    n_slots = up_table.shape[0]
    cap_tokens = max(1, 2 ** 23 // (sel_tok * width))
    block_tok = math.gcd(tok_dev, 2 ** int(math.log2(cap_tokens)))
    n_blocks = tok_dev // block_tok

    def scan_step(acc_pair, block_in):
        acc_up, acc_down = acc_pair
        x_blk, slot_blk, gate_blk, dy_blk = block_in
        up_rows = up_table[slot_blk]
        down_rows = down_table[slot_blk]
        pre_act = jnp.einsum('bsd,bd->bs', up_rows, x_blk, preferred_element_type=jnp.float32)
        act_val, slope_val = gelu_pair(pre_act)
        w_out = (gate_blk * act_val).astype(jnp.bfloat16)
        y_blk = jnp.einsum('bs,bsd->bd', w_out, down_rows, preferred_element_type=jnp.float32).astype(jnp.bfloat16)
        back_dot = jnp.einsum('bsd,bd->bs', down_rows, dy_blk, preferred_element_type=jnp.float32)
        coef_bf = (gate_blk * slope_val * back_dot).astype(jnp.bfloat16)
        dx_blk = jnp.einsum('bs,bsd->bd', coef_bf, up_rows, preferred_element_type=jnp.float32).astype(jnp.bfloat16)
        flat_slots = slot_blk.reshape(-1)
        up_part = coef_bf.astype(jnp.float32)[:, :, None] * x_blk[:, None, :]
        down_part = w_out.astype(jnp.float32)[:, :, None] * dy_blk[:, None, :]
        acc_up = acc_up.at[flat_slots].add(up_part.reshape(-1, width))
        acc_down = acc_down.at[flat_slots].add(down_part.reshape(-1, width))
        return (acc_up, acc_down), (y_blk, dx_blk)

    zero_acc = jnp.zeros((n_slots, width), jnp.float32)
    blocks_in = (tokens.reshape(n_blocks, block_tok, width), slot_flat.reshape(n_blocks, block_tok, sel_tok), gate_flat.reshape(n_blocks, block_tok, sel_tok), grad_out.reshape(n_blocks, block_tok, width))
    (acc_up, acc_down), (y_all, dx_all) = lax.scan(scan_step, (zero_acc, zero_acc), blocks_in)
    return acc_up, acc_down, y_all.reshape(tok_dev, width), dx_all.reshape(tok_dev, width)


def solution(mesh):
    n_group = mesh.shape['ep']
    tok_spec = P(('dp', 'ep'))
    table_spec = P('ep')

    def per_device(tokens, slot_ids, request_rows, gate_vals, grad_out, up_local, down_local):
        tok_dev, width = tokens.shape
        rows_owner = up_local.shape[0]
        n_req = request_rows.shape[2]
        sel_tok = slot_ids.shape[1] * slot_ids.shape[2]
        asked_rows = lax.all_to_all(request_rows[0], 'ep', 0, 0, tiled=True)
        up_pulled = lax.all_to_all(up_local[asked_rows], 'ep', 0, 0, tiled=True).reshape(n_group * n_req, width)
        down_pulled = lax.all_to_all(down_local[asked_rows], 'ep', 0, 0, tiled=True).reshape(n_group * n_req, width)
        acc_up, acc_down, y_local, dx_local = local_layer(tokens, slot_ids.reshape(tok_dev, sel_tok), gate_vals.reshape(tok_dev, sel_tok), grad_out, up_pulled, down_pulled)
        back_up = lax.all_to_all(acc_up.astype(jnp.bfloat16).reshape(n_group, n_req, width), 'ep', 0, 0, tiled=True)
        back_down = lax.all_to_all(acc_down.astype(jnp.bfloat16).reshape(n_group, n_req, width), 'ep', 0, 0, tiled=True)
        flat_asked = asked_rows.reshape(-1)
        grad_up = jax.ops.segment_sum(back_up.reshape(-1, width).astype(jnp.float32), flat_asked, num_segments=rows_owner)
        grad_down = jax.ops.segment_sum(back_down.reshape(-1, width).astype(jnp.float32), flat_asked, num_segments=rows_owner)
        return y_local, dx_local, grad_up.astype(jnp.bfloat16), grad_down.astype(jnp.bfloat16)

    return jax.shard_map(per_device, mesh=mesh, in_specs=(tok_spec, tok_spec, tok_spec, tok_spec, tok_spec, table_spec, table_spec), out_specs=(tok_spec, tok_spec, tok_spec, tok_spec), check_vma=False)
```

profile of v0, /device:TPU:81, one launch (start us, length us, event | category | flops | bytes accessed | tf_op | source)
XLA Modules:
  0.0 778.2 jit_solution(17919522337771640902)
XLA Ops:
  0.6 10.4 %all_to_all.32 = s32[8,1,128]{2,1,0:T(1,128)S(1)} all-to-all(s32[8,1,128]{2,1,0:T(1,128)} %bitcast.152), channel_id=1, replica_groups=mesh['dp'=4,'ep'=8] {'ep'}, dimensions={0} | all-to-all | bytes 8192 | tf_op jit(solution)/shard_map/all_to_all | solution.py:57
  11.7 13.3 %gather_fusion.3 = bf16[1024,2048]{1,0:T(8,128)(2,1)} fusion(bf16[2048,2048]{1,0:T(8,128)(2,1)} %param.15, s32[1024]{0:T(1024)S(1)} %fusion.29), kind=kCustom, calls=%fused_computation.3 | custom fusion | bytes 8392704 | tf_op jit(solution)/shard_map/gather | solution.py:59
  30.1 13.3 %gather_fusion.2 = bf16[1024,2048]{1,0:T(8,128)(2,1)} fusion(bf16[2048,2048]{1,0:T(8,128)(2,1)} %param.14, s32[1024]{0:T(1024)S(1)} %fusion.29), kind=kCustom, calls=%fused_computation.2 | custom fusion | bytes 8392704 | tf_op jit(solution)/shard_map/gather | solution.py:58
  43.4 35.4 %all-to-all-done.2 = bf16[8,128,2048]{2,1,0:T(8,128)(2,1)} async-done(((bf16[8,128,2048]{2,1,0:T(8,128)(2,1)}), bf16[8,128,2048]{2,1,0:T(8,128)(2,1)}, u32[]{:S(2)}, u32[]{:S(2)}) %all-to-all-start.2) | async-done | bytes 4194336 | tf_op jit(solution)/shard_map/all_to_all | solution.py:59
  84.7 48.2 %all-to-all-done.1 = bf16[8,128,2048]{2,1,0:T(8,128)(2,1)} async-done(((bf16[8,128,2048]{2,1,0:T(8,128)(2,1)}), bf16[8,128,2048]{2,1,0:T(8,128)(2,1)}, u32[]{:S(2)}, u32[]{:S(2)}) %all-to-all-start.1) | async-done | bytes 4194336 | tf_op jit(solution)/shard_map/all_to_all | solution.py:58
  141.9 491.3 %while.16 = (s32[]{:T(128)}, f32[1024,2048]{1,0:T(8,128)}, f32[1024,2048]{1,0:T(8,128)}, bf16[2,32,2048]{2,1,0:T(8,128)(2,1)}, bf16[2,32,2048]{2,1,0:T(8,128)(2,...) while((s32[]{:T(128)}, f32[1024,2048]{1,0:T(8,128)}, ...), condition=%wide.region_3.4_spmd, body=%wide.region_0.3_spmd.sunk | while | flops 100888576 | bytes 456458624 | solution.py:43
  161.1 34.1 %gather_fusion.1 = bf16[4096,2048]{1,0:T(8,128)(2,1)} fusion(bf16[1024,2048]{1,0:T(8,128)(2,1)} %get-tuple-element.234, s32[4096]{0:T(1024)S(1)} %get-tuple-element.189), kind=kCustom, calls=%fused_computation.1.clone.1 | custom fusion | bytes 33570816 | tf_op jit(solution)/shard_map/while/body/eval_jaxpr/gather | solution.py:26
  203.2 34.1 %gather_fusion = bf16[4096,2048]{1,0:T(8,128)(2,1)} fusion(bf16[1024,2048]{1,0:T(8,128)(2,1)} %get-tuple-element.232, s32[4096]{0:T(1024)S(1)} %get-tuple-element.189), kind=kCustom, calls=%fused_computation.clone.1 | custom fusion | bytes 33570816 | tf_op jit(solution)/shard_map/while/body/eval_jaxpr/gather | solution.py:25
  245.5 8.2 %fusion.62 = bf16[32,1,2048]{2,1,0:T(2,128)(2,1)S(1)} fusion(bf16[32,128,2048]{2,1,0:T(8,128)(2,1)} %bitcast.135, bf16[32,128,1]{1,0,2:T(8,128)(2,1)S(1)} %bitcast.143), kind=kOutput, calls=%fused_computation.38.clone.1 | convolution fusion | flops 16777216 | bytes 16916480 | tf_op jit(solution)/shard_map/while/body/eval_jaxpr/bs,bsd->bd/dot_general | solution.py:33
  256.9 21.4 %bitcast_multiply_fusion.4 = (f32[4096,2048]{1,0:T(8,128)}, f32[4096,2048]{1,0:T(8,128)}) fusion(f32[32,2048]{1,0:T(8,128)S(1)} %get-tuple-element.188, f32[4096]{0:T(1024)S(1)} %get-tuple-element.192, f32[32,2048]{1,0:T(8,128)S(1)} %get-tuple-element.193, f32[4096]{0:T(1024)S(1)} %get-tuple-element.194), kind=kLoop, calls=%fused_computation.8.clone.1 | loop fusion | flops 16777216 | bytes 67665920 | tf_op jit(solution)/shard_map/while/body/eval_jaxpr/mul | solution.py:36
  278.4 58.7 %scatter_fusion = f32[1024,2048]{1,0:T(8,128)} fusion(f32[1024,2048]{1,0:T(8,128)} %get-tuple-element.214, s32[4096]{0:T(1024)S(1)} %bitcast.140, f32[4096,2048]{1,0:T(8,128)} %get-tuple-element.195), kind=kCustom, calls=%fused_computation.4.clone.1 | custom fusion | flops 8388608 | bytes 100679680 | tf_op jit(solution)/shard_map/while/body/eval_jaxpr/scatter-add | solution.py:37
  337.1 58.8 %scatter_fusion.1 = f32[1024,2048]{1,0:T(8,128)} fusion(f32[1024,2048]{1,0:T(8,128)} %get-tuple-element.215, s32[4096]{0:T(1024)S(1)} %bitcast.141, f32[4096,2048]{1,0:T(8,128)} %get-tuple-element.196), kind=kCustom, calls=%fused_computation.5.clone.1 | custom fusion | flops 8388608 | bytes 100679680 | tf_op jit(solution)/shard_map/while/body/eval_jaxpr/scatter-add | solution.py:38
  398.4 34.1 %gather_fusion.1 = bf16[4096,2048]{1,0:T(8,128)(2,1)} fusion(bf16[1024,2048]{1,0:T(8,128)(2,1)} %get-tuple-element.234, s32[4096]{0:T(1024)S(1)} %get-tuple-element.189), kind=kCustom, calls=%fused_computation.1.clone.1 | custom fusion | bytes 33570816 | tf_op jit(solution)/shard_map/while/body/eval_jaxpr/gather | solution.py:26
  440.5 34.1 %gather_fusion = bf16[4096,2048]{1,0:T(8,128)(2,1)} fusion(bf16[1024,2048]{1,0:T(8,128)(2,1)} %get-tuple-element.232, s32[4096]{0:T(1024)S(1)} %get-tuple-element.189), kind=kCustom, calls=%fused_computation.clone.1 | custom fusion | bytes 33570816 | tf_op jit(solution)/shard_map/while/body/eval_jaxpr/gather | solution.py:25
  482.8 8.2 %fusion.62 = bf16[32,1,2048]{2,1,0:T(2,128)(2,1)S(1)} fusion(bf16[32,128,2048]{2,1,0:T(8,128)(2,1)} %bitcast.135, bf16[32,128,1]{1,0,2:T(8,128)(2,1)S(1)} %bitcast.143), kind=kOutput, calls=%fused_computation.38.clone.1 | convolution fusion | flops 16777216 | bytes 16916480 | tf_op jit(solution)/shard_map/while/body/eval_jaxpr/bs,bsd->bd/dot_general | solution.py:33
  494.2 21.4 %bitcast_multiply_fusion.4 = (f32[4096,2048]{1,0:T(8,128)}, f32[4096,2048]{1,0:T(8,128)}) fusion(f32[32,2048]{1,0:T(8,128)S(1)} %get-tuple-element.188, f32[4096]{0:T(1024)S(1)} %get-tuple-element.192, f32[32,2048]{1,0:T(8,128)S(1)} %get-tuple-element.193, f32[4096]{0:T(1024)S(1)} %get-tuple-element.194), kind=kLoop, calls=%fused_computation.8.clone.1 | loop fusion | flops 16777216 | bytes 67665920 | tf_op jit(solution)/shard_map/while/body/eval_jaxpr/mul | solution.py:36
  515.6 58.7 %scatter_fusion = f32[1024,2048]{1,0:T(8,128)} fusion(f32[1024,2048]{1,0:T(8,128)} %get-tuple-element.214, s32[4096]{0:T(1024)S(1)} %bitcast.140, f32[4096,2048]{1,0:T(8,128)} %get-tuple-element.195), kind=kCustom, calls=%fused_computation.4.clone.1 | custom fusion | flops 8388608 | bytes 100679680 | tf_op jit(solution)/shard_map/while/body/eval_jaxpr/scatter-add | solution.py:37
  574.4 58.8 %scatter_fusion.1 = f32[1024,2048]{1,0:T(8,128)} fusion(f32[1024,2048]{1,0:T(8,128)} %get-tuple-element.215, s32[4096]{0:T(1024)S(1)} %bitcast.141, f32[4096,2048]{1,0:T(8,128)} %get-tuple-element.196), kind=kCustom, calls=%fused_computation.5.clone.1 | custom fusion | flops 8388608 | bytes 100679680 | tf_op jit(solution)/shard_map/while/body/eval_jaxpr/scatter-add | solution.py:38
  650.7 42.6 %all-to-all-done.4 = bf16[8,128,2048]{2,1,0:T(8,128)(2,1)} async-done(((bf16[8,128,2048]{2,1,0:T(8,128)(2,1)}), bf16[8,128,2048]{2,1,0:T(8,128)(2,1)}, u32[]{:S(2)}, u32[]{:S(2)}) %all-to-all-start.4) | async-done | bytes 4194336 | tf_op jit(solution)/shard_map/all_to_all | solution.py:62
  698.9 21.4 %scatter_custom_fusion.3 = f32[2048,2048]{1,0:T(8,128)} fusion(s32[1024]{0:T(1024)} %bitcast.150, bf16[1024,2048]{1,0:T(8,128)(2,1)} %bitcast.44, f32[]{:T(128)} %constant.9.clone.1), kind=kCustom, calls=%fused_computation.46 | custom fusion | flops 4194304 | bytes 20972032 | tf_op jit(solution)/shard_map/scatter-add | solution.py:65
  720.2 9.2 %convert_element_type.61 = bf16[2048,2048]{1,0:T(8,128)(2,1)} convert(f32[2048,2048]{1,0:T(8,128)} %scatter_custom_fusion.3) | non-fusion elementwise | flops 4194304 | bytes 25165824 | tf_op jit(solution)/shard_map/convert_element_type | solution.py:66
  729.5 18.0 %all-to-all-done.3 = bf16[8,128,2048]{2,1,0:T(8,128)(2,1)} async-done(((bf16[8,128,2048]{2,1,0:T(8,128)(2,1)}), bf16[8,128,2048]{2,1,0:T(8,128)(2,1)}, u32[]{:S(2)}, u32[]{:S(2)}) %all-to-all-start.3) | async-done | bytes 4194336 | tf_op jit(solution)/shard_map/all_to_all | solution.py:61
  747.5 21.4 %scatter_custom_fusion.2 = f32[2048,2048]{1,0:T(8,128)} fusion(s32[1024]{0:T(1024)} %bitcast.151, bf16[1024,2048]{1,0:T(8,128)(2,1)} %bitcast.43, f32[]{:T(128)} %constant.9.clone.1), kind=kCustom, calls=%fused_computation.48 | custom fusion | flops 4194304 | bytes 20972032 | tf_op jit(solution)/shard_map/scatter-add | solution.py:64
  768.9 9.0 %convert_element_type.57 = bf16[2048,2048]{1,0:T(8,128)(2,1)} convert(f32[2048,2048]{1,0:T(8,128)} %scatter_custom_fusion.2) | non-fusion elementwise | flops 4194304 | bytes 25165824 | tf_op jit(solution)/shard_map/convert_element_type | solution.py:66
  (73 shorter events, 87.4 us)
Async XLA Ops:
  11.1 0.6 copy-start.6
  24.9 53.8 %all-to-all-start.2 = ((bf16[8,128,2048]{2,1,0:T(8,128)(2,1)}), bf16[8,128,2048]{2,1,0:T(8,128)(2,1)}, u32[]{:S(2)}, u32[]{:S(2)}) async-start(bf16[8,128,2048]{2,1,0:T(8,128)(2,1)} %bitcast.139), calls=%async_computation.2 | async-start | bytes 8388608 | tf_op jit(solution)/shard_map/all_to_all | solution.py:59
  43.4 40.9 %copy-start.4 = (s32[64,4,32]{0,2,1:T(8,128)S(1)}, s32[64,4,32]{0,2,1:T(8,128)}, u32[]{:S(2)}) copy-start(s32[64,4,32]{0,2,1:T(8,128)} %param.10) | copy-start | bytes 98308
  43.4 41.1 %copy-start.5 = (f32[64,4,32]{0,2,1:T(8,128)S(1)}, f32[64,4,32]{0,2,1:T(8,128)}, u32[]{:S(2)}) copy-start(f32[64,4,32]{0,2,1:T(8,128)} %param.12) | copy-start | bytes 98308
  78.8 54.2 %all-to-all-start.1 = ((bf16[8,128,2048]{2,1,0:T(8,128)(2,1)}), bf16[8,128,2048]{2,1,0:T(8,128)(2,1)}, u32[]{:S(2)}, u32[]{:S(2)}) async-start(bf16[8,128,2048]{2,1,0:T(8,128)(2,1)} %bitcast.136), calls=%async_computation.1 | async-start | bytes 8388608 | tf_op jit(solution)/shard_map/all_to_all | solution.py:58
  158.6 0.6 copy-start
  158.6 86.9 %copy-start.2 = (f32[2,32,128]{2,1,0:T(8,128)}, f32[2,32,128]{2,1,0:T(8,128)S(1)}, u32[]{:S(2)}) copy-start(f32[2,32,128]{2,1,0:T(8,128)S(1)} %get-tuple-element.231) | copy-start | bytes 98308 | tf_op jit(solution)/shard_map/while
  237.3 16.5 %slice-start = ((s8[16777216]{0:T(1024)(128)(4,1)}), s8[4194304]{0:T(1024)(128)(4,1)S(1)}, s32[]{:S(2)}) async-start(s8[16777216]{0:T(1024)(128)(4,1)} %bitcast.131), calls=%async_computation.5 | async-start | bytes 8388608 | tf_op jit(solution)/shard_map/while
  237.3 16.5 %slice-start.1 = ((s8[16777216]{0:T(1024)(128)(4,1)}), s8[4194304]{0:T(1024)(128)(4,1)S(1)}, s32[]{:S(2)}) async-start(s8[16777216]{0:T(1024)(128)(4,1)} %bitcast.131), calls=%async_computation.6 | async-start | bytes 8388608 | tf_op jit(solution)/shard_map/while
  237.3 16.5 %slice-start.2 = ((s8[16777216]{0:T(1024)(128)(4,1)}), s8[4194304]{0:T(1024)(128)(4,1)S(1)}, s32[]{:S(2)}) async-start(s8[16777216]{0:T(1024)(128)(4,1)} %bitcast.131), calls=%async_computation.7 | async-start | bytes 8388608 | tf_op jit(solution)/shard_map/while
  245.5 8.3 %slice-start.3 = ((s8[16777216]{0:T(1024)(128)(4,1)}), s8[4194304]{0:T(1024)(128)(4,1)S(1)}, s32[]{:S(2)}) async-start(s8[16777216]{0:T(1024)(128)(4,1)} %bitcast.131), calls=%async_computation.8 | async-start | bytes 8388608 | tf_op jit(solution)/shard_map/while
  337.1 58.8 %copy-start.1 = (s32[2,32,128]{2,1,0:T(8,128)S(1)}, s32[2,32,128]{2,1,0:T(8,128)}, u32[]{:S(2)}) copy-start(s32[2,32,128]{2,1,0:T(8,128)} %copy-done) | copy-start | bytes 98308 | tf_op jit(solution)/shard_map/while
  337.1 58.8 %copy-start.3 = (f32[2,32,128]{2,1,0:T(8,128)S(1)}, f32[2,32,128]{2,1,0:T(8,128)}, u32[]{:S(2)}) copy-start(f32[2,32,128]{2,1,0:T(8,128)} %copy-done.2) | copy-start | bytes 98308 | tf_op jit(solution)/shard_map/while
  395.9 0.6 copy-start
  395.9 86.9 %copy-start.2 = (f32[2,32,128]{2,1,0:T(8,128)}, f32[2,32,128]{2,1,0:T(8,128)S(1)}, u32[]{:S(2)}) copy-start(f32[2,32,128]{2,1,0:T(8,128)S(1)} %get-tuple-element.231) | copy-start | bytes 98308 | tf_op jit(solution)/shard_map/while
  474.6 16.5 %slice-start = ((s8[16777216]{0:T(1024)(128)(4,1)}), s8[4194304]{0:T(1024)(128)(4,1)S(1)}, s32[]{:S(2)}) async-start(s8[16777216]{0:T(1024)(128)(4,1)} %bitcast.131), calls=%async_computation.5 | async-start | bytes 8388608 | tf_op jit(solution)/shard_map/while
  474.6 16.5 %slice-start.1 = ((s8[16777216]{0:T(1024)(128)(4,1)}), s8[4194304]{0:T(1024)(128)(4,1)S(1)}, s32[]{:S(2)}) async-start(s8[16777216]{0:T(1024)(128)(4,1)} %bitcast.131), calls=%async_computation.6 | async-start | bytes 8388608 | tf_op jit(solution)/shard_map/while
  474.6 16.5 %slice-start.2 = ((s8[16777216]{0:T(1024)(128)(4,1)}), s8[4194304]{0:T(1024)(128)(4,1)S(1)}, s32[]{:S(2)}) async-start(s8[16777216]{0:T(1024)(128)(4,1)} %bitcast.131), calls=%async_computation.7 | async-start | bytes 8388608 | tf_op jit(solution)/shard_map/while
  482.8 8.3 %slice-start.3 = ((s8[16777216]{0:T(1024)(128)(4,1)}), s8[4194304]{0:T(1024)(128)(4,1)S(1)}, s32[]{:S(2)}) async-start(s8[16777216]{0:T(1024)(128)(4,1)} %bitcast.131), calls=%async_computation.8 | async-start | bytes 8388608 | tf_op jit(solution)/shard_map/while
  574.4 58.8 %copy-start.1 = (s32[2,32,128]{2,1,0:T(8,128)S(1)}, s32[2,32,128]{2,1,0:T(8,128)}, u32[]{:S(2)}) copy-start(s32[2,32,128]{2,1,0:T(8,128)} %copy-done) | copy-start | bytes 98308 | tf_op jit(solution)/shard_map/while
  574.4 58.8 %copy-start.3 = (f32[2,32,128]{2,1,0:T(8,128)S(1)}, f32[2,32,128]{2,1,0:T(8,128)}, u32[]{:S(2)}) copy-start(f32[2,32,128]{2,1,0:T(8,128)} %copy-done.2) | copy-start | bytes 98308 | tf_op jit(solution)/shard_map/while
  639.1 54.2 %all-to-all-start.4 = ((bf16[8,128,2048]{2,1,0:T(8,128)(2,1)}), bf16[8,128,2048]{2,1,0:T(8,128)(2,1)}, u32[]{:S(2)}, u32[]{:S(2)}) async-start(bf16[8,128,2048]{2,1,0:T(8,128)(2,1)} %bitcast.138), calls=%async_computation.4 | async-start | bytes 8388608 | tf_op jit(solution)/shard_map/all_to_all | solution.py:62
  693.3 54.2 %all-to-all-start.3 = ((bf16[8,128,2048]{2,1,0:T(8,128)(2,1)}), bf16[8,128,2048]{2,1,0:T(8,128)(2,1)}, u32[]{:S(2)}, u32[]{:S(2)}) async-start(bf16[8,128,2048]{2,1,0:T(8,128)(2,1)} %bitcast.137), calls=%async_computation.3 | async-start | bytes 8388608 | tf_op jit(solution)/shard_map/all_to_all | solution.py:61
where the time goes:
time: 784 us; the launch traced here: 778 us
  other arithmetic  355 us (45%)
  local copies, waits for them, and re-layouts  176 us (22%)
  waiting for transfers between devices  144 us (18%)
  matrix products  53.5 us (7%)
  starting transfers between devices  21.7 us (3%)
  loops' own time  16.9 us (2%)
  blocking collectives  10.4 us (1%)
    scatter-add x2, other arithmetic, scan_step(): acc_down = acc_down.at[flat_slots].add(down_part.reshape(-1, width))  118 us
    scatter-add x2, other arithmetic, scan_step(): acc_up = acc_up.at[flat_slots].add(up_part.reshape(-1, width))  117 us
    gather x2, local copies, waits for them, and re-layouts, scan_step(): up_rows = up_table[slot_blk]  68.2 us
    gather x2, local copies, waits for them, and re-layouts, scan_step(): down_rows = down_table[slot_blk]  68.1 us
    all_to_all x1, waiting for transfers between devices, per_device(): lax.all_to_all(up_local[asked_rows], 'ep', 0, 0, tiled=True)  48.2 us
    mul x4, other arithmetic, scan_step(): down_part = w_out.astype(jnp.float32)[:, :, None] * dy_blk[:, None, :]  42.9 us
    all_to_all x1, waiting for transfers between devices, per_device(): lax.all_to_all(acc_down.astype(jnp.bfloat16).reshape(n_group, n_req, widt...  42.6 us
    all_to_all x1, waiting for transfers between devices, per_device(): lax.all_to_all(down_local[asked_rows], 'ep', 0, 0, tiled=True)  35.4 us
  transfers between devices with their start and end apart: 4, of which 4 were waited for; matrix products, arithmetic and copies ran while one was open for 6% of the time, Pallas kernels for 0%

commit v1 on v0

v1 whole, which is shorter than its diff:
```python
import functools
import math

import jax
import jax.numpy as jnp
from jax import lax
from jax.experimental import pallas as pl
from jax.experimental.pallas import tpu as pltpu
from jax.sharding import PartitionSpec as P

MESH = pl.DeviceIdType.MESH
F32 = jnp.float32
BF16 = jnp.bfloat16
NT = (((1,), (1,)), ((), ()))
OWN, RIGHT, FAR, LEFT = 0, 1, 2, 3
COLS = 512


def gelu_pair(pre_act):
    normal_cdf = 0.5 * (1.0 + lax.erf(pre_act * (2.0 ** -0.5)))
    normal_pdf = jnp.exp(-0.5 * pre_act * pre_act) * ((2.0 * math.pi) ** -0.5)
    return pre_act * normal_cdf, normal_cdf + pre_act * normal_pdf


def exchange_kernel(x_ref, dy_ref, slot_ref, gate_ref, req_ref, u_hbm, v_hbm,
                    nearp_out, nearm_out, own_out, xall_out, dyall_out, wc_out, rows_out,
                    u_v, v_v, ureq, vreq, onehot, xa, da, gall, qall, gmix, gloc, part, sib, far,
                    load_sem, out_sem, q_send, q_recv, g_send, g_recv, ax_send, ax_recv, d2d_send, d2d_recv,
                    p_send, p_recv, f_send, f_recv):
    n_dev = req_ref.shape[0]
    n_req = req_ref.shape[1]
    n_chip = n_dev // 2
    n_tok, width = x_ref.shape
    n_rows = u_v.shape[0]
    me = lax.axis_index('ep')
    core = lax.rem(me, 2)
    chip = me // 2
    other = 1 - core

    shift = n_req.bit_length() - 1

    def dev(rel, which):
        return lax.rem(chip + rel, n_chip) * 2 + which

    right, left, mate = dev(RIGHT, core), dev(LEFT, core), dev(OWN, other)
    peers = [(rel, flip) for rel in range(4) for flip in range(2) if (rel, flip) != (0, 0)]

    def peer_core(flip):
        return core if flip == 0 else other

    barrier = pltpu.get_barrier_semaphore()
    for rel, flip in peers:
        pl.semaphore_signal(barrier, inc=1, device_id={'ep': dev(rel, peer_core(flip))}, device_id_type=MESH)
    pl.semaphore_wait(barrier, len(peers))

    def rcopy(src, dst, s_sem, r_sem, target):
        return pltpu.make_async_remote_copy(src_ref=src, dst_ref=dst, send_sem=s_sem, recv_sem=r_sem, device_id={'ep': target}, device_id_type=MESH)

    load_u = pltpu.make_async_copy(u_hbm, u_v, load_sem.at[0])
    load_v = pltpu.make_async_copy(v_hbm, v_v, load_sem.at[1])

    q_copies = {}
    for n, (rel, flip) in enumerate(peers):
        back = (4 - rel) % 4
        q_copies[rel, flip] = rcopy(req_ref, qall.at[back, core], q_send.at[n], q_recv.at[n], dev(rel, peer_core(flip)))
        q_copies[rel, flip].start()
    x_right = rcopy(x_ref, xa.at[LEFT, core], ax_send.at[0], ax_recv.at[0], right)
    d_left = rcopy(dy_ref, da.at[RIGHT, core], ax_send.at[1], ax_recv.at[1], left)
    d_right = rcopy(dy_ref, da.at[LEFT, core], ax_send.at[2], ax_recv.at[2], right)
    x_left = rcopy(x_ref, xa.at[RIGHT, core], ax_send.at[3], ax_recv.at[3], left)
    x_far = rcopy(xa.at[LEFT, core], xa.at[FAR, core], ax_send.at[4], ax_recv.at[4], right)
    d_far = rcopy(da.at[RIGHT, core], da.at[FAR, core], ax_send.at[5], ax_recv.at[5], left)
    x_right.start()
    d_left.start()
    load_u.start()
    load_v.start()
    x_mate = [rcopy(x_ref if rel == OWN else xa.at[rel, core], xa.at[rel, core], d2d_send.at[rel, 0], d2d_recv.at[rel, 0], mate) for rel in range(4)]
    d_mate = [rcopy(dy_ref if rel == OWN else da.at[rel, core], da.at[rel, core], d2d_send.at[rel, 1], d2d_recv.at[rel, 1], mate) for rel in range(4)]
    x_mate[OWN].start()
    d_mate[OWN].start()
    xa[OWN, core] = x_ref[...]
    da[OWN, core] = dy_ref[...]

    own_iota = lax.broadcasted_iota(jnp.int32, (n_dev, n_req), 0)
    sub_iota = lax.broadcasted_iota(jnp.int32, (n_req, n_req), 0)

    def gate_step(step, carry):
        base = pl.multiple_of(step * 8, 8)
        s_blk = slot_ref[pl.ds(base, 8), :]
        g_blk = gate_ref[pl.ds(base, 8), :]
        for j in range(8):
            s_row = s_blk[j:j + 1, :]
            g_row = g_blk[j:j + 1, :]
            spread = jnp.where(own_iota == (s_row >> shift), g_row, 0.0)
            hi = spread.astype(BF16).astype(F32)
            rest = spread - hi
            mid = rest.astype(BF16).astype(F32)
            lo = rest - mid
            lhs = jnp.concatenate([hi, mid, lo], axis=0).astype(BF16)
            hot = jnp.where(sub_iota == (s_row & (n_req - 1)), 1.0, 0.0).astype(BF16)
            res = lax.dot_general(lhs, hot, NT, preferred_element_type=F32)
            start = pl.multiple_of((base + j) * n_dev, n_dev)
            gmix[pl.ds(start, n_dev), :] = res[0:n_dev] + res[n_dev:2 * n_dev] + res[2 * n_dev:3 * n_dev]
        return carry

    lax.fori_loop(0, n_tok // 8, gate_step, 0)
    for o in range(n_dev):
        gloc[o] = gmix[pl.ds(o, n_tok, stride=n_dev), :]

    x_right.wait_recv()
    x_far.start()
    d_left.wait_recv()
    d_far.start()
    g_copies = {}
    for n, (rel, flip) in enumerate(peers):
        back = (4 - rel) % 4
        target = dev(rel, peer_core(flip))
        g_copies[rel, flip] = rcopy(gloc.at[target], gall.at[back, core], g_send.at[n], g_recv.at[n], target)
        g_copies[rel, flip].start()
    gall[OWN, core] = gloc[me]
    d_right.start()
    x_left.start()
    x_mate[LEFT].start()
    d_mate[RIGHT].start()

    for rel, flip in peers:
        q_copies[rel, flip].wait_recv()
    qall[OWN, core] = req_ref[...]
    row_list = [qall[rel, which, pl.ds(me, 1), :] for rel in range(4) for which in range(2)]
    rows_mat = jnp.concatenate(row_list, axis=0)
    rows_out[...] = rows_mat
    rows_col = jnp.transpose(jnp.concatenate([rows_mat.astype(F32)] * (n_req // n_dev), axis=0))
    load_u.wait()
    load_v.wait()
    lane_iota = lax.broadcasted_iota(jnp.int32, (n_req, n_req), 1).astype(F32)

    def gather(rel):
        for which in range(2):
            col = jnp.broadcast_to(rows_col[:, rel * 2 + which:rel * 2 + which + 1], (n_req, n_req))
            for blk in range(n_rows // n_req):
                onehot[pl.ds(which * n_req, n_req), pl.ds(blk * n_req, n_req)] = jnp.where(col - blk * n_req == lane_iota, 1.0, 0.0).astype(BF16)

        def body(step, carry):
            cols = pl.ds(pl.multiple_of(step * COLS, COLS), COLS)
            ureq[rel, :, cols] = jnp.dot(onehot[...], u_v[:, cols], preferred_element_type=F32).astype(BF16)
            vreq[rel, :, cols] = jnp.dot(onehot[...], v_v[:, cols], preferred_element_type=F32).astype(BF16)
            return carry

        lax.fori_loop(0, width // COLS, body, 0)

    zeros = jnp.zeros((n_tok, n_req), BF16)

    def chunk(rel):
        x_blk = xa[rel].reshape(2 * n_tok, width)
        pre = lax.dot_general(x_blk, ureq[rel], NT, preferred_element_type=F32)
        dy_blk = da[rel].reshape(2 * n_tok, width)
        back_dot = lax.dot_general(dy_blk, vreq[rel], NT, preferred_element_type=F32)
        for which in range(2):
            t_lo, s_lo = which * n_tok, which * n_req
            act, slope = gelu_pair(pre[t_lo:t_lo + n_tok, s_lo:s_lo + n_req])
            gate = gall[rel, which]
            w_blk = (gate * act).astype(BF16)
            c_blk = (gate * slope * back_dot[t_lo:t_lo + n_tok, s_lo:s_lo + n_req]).astype(BF16)
            z_lo = (1 - which) * n_req
            wc_out[rel, pl.ds(t_lo, n_tok), pl.ds(s_lo, n_req)] = w_blk
            wc_out[rel, pl.ds(t_lo, n_tok), pl.ds(z_lo, n_req)] = zeros
            wc_out[rel, pl.ds(2 * n_tok + t_lo, n_tok), pl.ds(s_lo, n_req)] = c_blk
            wc_out[rel, pl.ds(2 * n_tok + t_lo, n_tok), pl.ds(z_lo, n_req)] = zeros

        def body(step, carry):
            cols = pl.ds(pl.multiple_of(step * COLS, COLS), COLS)
            part[rel, 0, :, cols] = jnp.dot(wc_out[rel, 0:2 * n_tok, :], vreq[rel, :, cols], preferred_element_type=F32)
            part[rel, 1, :, cols] = jnp.dot(wc_out[rel, 2 * n_tok:4 * n_tok, :], ureq[rel, :, cols], preferred_element_type=F32)
            return carry

        lax.fori_loop(0, width // COLS, body, 0)
        theirs = pl.ds(pl.multiple_of(other * n_tok, n_tok), n_tok)
        send = rcopy(part.at[rel, :, theirs, :], sib.at[rel], p_send.at[rel], p_recv.at[rel], mate)
        send.start()
        return send

    mine = pl.ds(pl.multiple_of(core * n_tok, n_tok), n_tok)

    def need(rel):
        for flip in range(2):
            if (rel, flip) != (0, 0):
                g_copies[(4 - rel) % 4, flip].wait_recv()
        x_mate[rel].wait_recv()
        d_mate[rel].wait_recv()

    def add_mate(rel, send):
        send.wait_recv()
        sib[rel] = sib[rel] + part[rel, :, mine, :]

    gather(FAR)
    gather(RIGHT)
    x_far.wait_recv()
    x_mate[FAR].start()
    d_far.wait_recv()
    d_mate[FAR].start()
    need(FAR)
    s_far = chunk(FAR)
    gather(LEFT)
    d_right.wait_recv()
    d_mate[LEFT].start()
    x_left.wait_recv()
    x_mate[RIGHT].start()
    add_mate(FAR, s_far)
    f_y = rcopy(sib.at[FAR, 0], far.at[0], f_send.at[0], f_recv.at[0], right)
    f_d = rcopy(sib.at[FAR, 1], far.at[1], f_send.at[1], f_recv.at[1], left)
    f_y.start()
    f_d.start()
    need(RIGHT)
    s_right = chunk(RIGHT)
    need(LEFT)
    s_left = chunk(LEFT)
    gather(OWN)
    need(OWN)
    s_own = chunk(OWN)
    o_x = pltpu.make_async_copy(xa, xall_out, out_sem.at[0])
    o_d = pltpu.make_async_copy(da, dyall_out, out_sem.at[1])
    o_x.start()
    o_d.start()
    add_mate(RIGHT, s_right)
    add_mate(LEFT, s_left)
    add_mate(OWN, s_own)
    o_own = pltpu.make_async_copy(sib.at[OWN], own_out, out_sem.at[2])
    o_own.start()
    f_y.wait_recv()
    sib[RIGHT, 0] = sib[RIGHT, 0] + far[0]
    o_right = pltpu.make_async_copy(sib.at[RIGHT], nearp_out, out_sem.at[3])
    o_right.start()
    f_d.wait_recv()
    sib[LEFT, 1] = sib[LEFT, 1] + far[1]
    o_left = pltpu.make_async_copy(sib.at[LEFT], nearm_out, out_sem.at[4])
    o_left.start()
    for key in q_copies:
        q_copies[key].wait_send()
        g_copies[key].wait_send()
    for copy in (x_right, d_left, d_right, x_left, x_far, d_far, *x_mate, *d_mate, s_far, s_right, s_left, s_own, f_y, f_d):
        copy.wait_send()
    for copy in (o_x, o_d, o_own, o_right, o_left):
        copy.wait()


def grad_kernel(rows_ref, wc_ref, xall_ref, dyall_ref, gu_ref, gv_ref, ct, wt):
    blk, width = gu_ref.shape
    n_rel = wc_ref.shape[0]
    n_tok2 = wc_ref.shape[1] // 2
    base = pl.program_id(0) * blk
    for rel in range(n_rel):
        rows = jnp.concatenate([rows_ref[2 * rel:2 * rel + 1, :], rows_ref[2 * rel + 1:2 * rel + 2, :]], axis=1)
        place = jnp.where(lax.broadcasted_iota(jnp.int32, (blk, rows.shape[1]), 0) + base == rows, 1.0, 0.0).astype(BF16)
        coef = lax.dot_general(place, wc_ref[rel], NT, preferred_element_type=F32).astype(BF16)
        wt[:, rel * n_tok2:(rel + 1) * n_tok2] = coef[:, :n_tok2]
        ct[:, rel * n_tok2:(rel + 1) * n_tok2] = coef[:, n_tok2:]
    for step in range(width // COLS):
        cols = pl.ds(step * COLS, COLS)
        gu_ref[:, cols] = jnp.dot(ct[...], xall_ref[:, cols], preferred_element_type=F32).astype(BF16)
        gv_ref[:, cols] = jnp.dot(wt[...], dyall_ref[:, cols], preferred_element_type=F32).astype(BF16)


def solution(mesh):
    n_dev = mesh.shape['ep']
    tok_spec = P(('dp', 'ep'))
    table_spec = P('ep')
    vmem = pl.BlockSpec(memory_space=pltpu.VMEM)
    hbm = pl.BlockSpec(memory_space=pl.ANY)
    dma = pltpu.SemaphoreType.DMA
    sds = jax.ShapeDtypeStruct

    def per_device(tokens, slot_ids, request_rows, gate_vals, grad_out, up_local, down_local):
        n_tok, width = tokens.shape
        n_rows = up_local.shape[0]
        n_req = request_rows.shape[2]
        sel = slot_ids.shape[1] * slot_ids.shape[2]
        n_all = n_dev * n_tok
        nearp, nearm, own, xall, dyall, wc, rows = pl.pallas_call(
            exchange_kernel,
            name='exchange',
            out_shape=(sds((2, n_tok, width), F32),) * 3 + (sds((4, 2, n_tok, width), BF16),) * 2 + (sds((4, 4 * n_tok, 2 * n_req), BF16), sds((n_dev, n_req), jnp.int32)),
            in_specs=[vmem] * 5 + [hbm] * 2,
            out_specs=(hbm,) * 5 + (vmem,) * 2,
            scratch_shapes=[
                pltpu.VMEM((n_rows, width), BF16), pltpu.VMEM((n_rows, width), BF16),
                pltpu.VMEM((4, 2 * n_req, width), BF16), pltpu.VMEM((4, 2 * n_req, width), BF16),
                pltpu.VMEM((2 * n_req, n_rows), BF16),
                pltpu.VMEM((4, 2, n_tok, width), BF16), pltpu.VMEM((4, 2, n_tok, width), BF16),
                pltpu.VMEM((4, 2, n_tok, n_req), F32), pltpu.VMEM((4, 2, n_dev, n_req), jnp.int32),
                pltpu.VMEM((n_tok * n_dev, n_req), F32), pltpu.VMEM((n_dev, n_tok, n_req), F32),
                pltpu.VMEM((4, 2, 2 * n_tok, width), F32), pltpu.VMEM((4, 2, n_tok, width), F32), pltpu.VMEM((2, n_tok, width), F32),
                dma((2,)), dma((5,)), dma((7,)), dma((7,)), dma((7,)), dma((7,)), dma((6,)), dma((6,)), dma((4, 2)), dma((4, 2)),
                dma((4,)), dma((4,)), dma((2,)), dma((2,)),
            ],
            compiler_params=pltpu.CompilerParams(collective_id=0, has_side_effects=True, vmem_limit_bytes=60 * 2 ** 20),
            cost_estimate=pl.CostEstimate(flops=4 * n_dev * n_req * n_rows * width, bytes_accessed=6 * n_rows * width, transcendentals=0),
        )(tokens, grad_out, slot_ids.reshape(n_tok, sel), gate_vals.reshape(n_tok, sel), request_rows[0], up_local, down_local)

        up_chip = [(d, (d + 2) % n_dev) for d in range(n_dev)]
        down_chip = [(d, (d - 2) % n_dev) for d in range(n_dev)]
        from_left = lax.ppermute(nearp, 'ep', up_chip)
        from_right = lax.ppermute(nearm, 'ep', down_chip)

        blk = min(256, n_rows)
        full = lambda shape: pl.BlockSpec(shape, lambda i: (0,) * len(shape))
        grad_up, grad_down = pl.pallas_call(
            grad_kernel,
            name='table_grads',
            out_shape=(sds((n_rows, width), BF16),) * 2,
            grid=(n_rows // blk,),
            in_specs=[full(rows.shape), full(wc.shape), full((n_all, width)), full((n_all, width))],
            out_specs=(pl.BlockSpec((blk, width), lambda i: (i, 0)),) * 2,
            scratch_shapes=[pltpu.VMEM((blk, n_all), BF16)] * 2,
            compiler_params=pltpu.CompilerParams(vmem_limit_bytes=40 * 2 ** 20),
            cost_estimate=pl.CostEstimate(flops=4 * n_rows * n_all * width, bytes_accessed=4 * (n_rows + n_all) * width, transcendentals=0),
        )(rows, wc, xall.reshape(n_all, width), dyall.reshape(n_all, width))
        total = (own + from_left + from_right).astype(BF16)
        return total[0], total[1], grad_up, grad_down

    return jax.shard_map(per_device, mesh=mesh, in_specs=(tok_spec, tok_spec, tok_spec, tok_spec, tok_spec, table_spec, table_spec), out_specs=(tok_spec, tok_spec, tok_spec, tok_spec), check_vma=False)
```

time: 784 us -> 82.7 us (0.11)
  other arithmetic: 355 us -> 0.18 us
  local copies, waits for them, and re-layouts: 176 us -> 8.81 us
  waiting for transfers between devices: 144 us -> 5.88 us
  Pallas kernels: 0 us -> 64.1 us
  matrix products: 53.5 us -> 0 us
  starting transfers between devices: 21.7 us -> 2.76 us
  loops' own time: 16.9 us -> 0 us
  blocking collectives: 10.4 us -> 0 us
    scatter-add x6 -> x0, other arithmetic: 278 us -> none  [the longest x2 118 us: scan_step(): acc_down = acc_down.at[flat_slots].add(down_part.reshape(-1, width))]
    gather x6 -> x0, local copies, waits for them, and re-layouts: 163 us -> none  [the longest x2 68.2 us: scan_step(): up_rows = up_table[slot_blk]]
    all_to_all x4 -> x0, waiting for transfers between devices: 144 us -> none  [the longest x1 48.2 us: per_device(): lax.all_to_all(up_local[asked_rows], 'ep', 0, 0, tiled=True)]
    pallas_call x0 -> x2, Pallas kernels: none -> 64.1 us  [the longest x1 51.3 us: per_device(): pl.pallas_call(exchange_kernel, name='exchange', out_shape=(sds((2, n_tok...]
    dot_general x8 -> x0, matrix products: 53.5 us -> none  [the longest x2 16.5 us: scan_step(): jnp.einsum('bs,bsd->bd', coef_bf, up_rows, preferred_element_type=jnp.flo...]
    mul x4 -> x0, other arithmetic: 42.9 us -> none  [scan_step(): down_part = w_out.astype(jnp.float32)[:, :, None] * dy_blk[:, None, :]]
    convert_element_type x6 -> x1, other arithmetic: 32.2 us -> 0.18 us  [per_device(): total = (own + from_left + from_right).astype(BF16)]
    all_to_all x4 -> x0, starting transfers between devices: 21.7 us -> none  [the longest x1 5.53 us: per_device(): lax.all_to_all(acc_up.astype(jnp.bfloat16).reshape(n_group, n_req, width)...]
  transfers between devices with their start and end apart: 4 -> 2, of which waited for: 4 -> 1; matrix products, arithmetic and copies ran while one was open for 6% -> 0% of each run, Pallas kernels for 0% -> 16%
where the time goes in v1:
time: 82.7 us; the launch traced here: 82.4 us
  Pallas kernels  64.1 us (78%)
  local copies, waits for them, and re-layouts  8.81 us (11%)
  waiting for transfers between devices  5.88 us (7%)
  starting transfers between devices  2.76 us (3%)
    pallas_call x1, Pallas kernels, per_device(): pl.pallas_call(exchange_kernel, name='exchange', out_shape=(sds((2, n_tok...  51.3 us
    pallas_call x1, Pallas kernels, per_device(): pl.pallas_call(grad_kernel, name='table_grads', out_shape=(sds((n_rows, w...  12.8 us
    ppermute x1, waiting for transfers between devices, per_device(): from_left = lax.ppermute(nearp, 'ep', up_chip)  5.88 us
    unnamed x10, local copies, waits for them, and re-layouts  4.91 us
    ppermute x1, starting transfers between devices, per_device(): from_right = lax.ppermute(nearm, 'ep', down_chip)  1.93 us
  transfers between devices with their start and end apart: 2, of which 1 were waited for; matrix products, arithmetic and copies ran while one was open for 0% of the time, Pallas kernels for 16%

profile of v1, /device:TPU:81, one launch (start us, length us, event | category | flops | bytes accessed | tf_op | source)
XLA Modules:
  0.0 82.4 jit_solution(7609175628423766768)
XLA Ops:
  0.6 1.5 %copy.13.slot_ref = s32[64,128]{1,0:T(8,128)} copy(s32[64,128]{0,1:T(8,128)} %bitcast.11) | data formatting | bytes 65536 | tf_op jit(solution)/shard_map/reshape | solution.py:297
  2.2 1.5 %copy.14.gate_ref = f32[64,128]{1,0:T(8,128)} copy(f32[64,128]{0,1:T(8,128)} %bitcast.12) | data formatting | bytes 65536 | tf_op jit(solution)/shard_map/reshape | solution.py:297
  3.7 51.3 %exchange.1 = (f32[2,64,2048]{2,1,0:T(8,128)}, f32[2,64,2048]{2,1,0:T(8,128)}, f32[2,64,2048]{2,1,0:T(8,128)}, bf16[4,2,64,2048]{3,2,1,0:T(8,128)(2,1)}, bf16[4,...) custom-call(bf16[64,2048]{1,0:T(8,128)(2,1)} %x_ref.1, bf16[64,2048]{1,0:T(8,128)(2,1)} %dy_ref.1, ...), custom_call_target="tpu_custom_call" | custom-call | flops 17179869184 | bytes 25165824 | tf_op jit(solution)/shard_map/exchange/pallas_call | solution.py:278
  55.0 0.8 %collective-permute-start = (f32[2,64,2048]{2,1,0:T(8,128)}, f32[2,64,2048]{2,1,0:T(8,128)S(1)}, u32[]{:S(2)}, u32[]{:S(2)}) collective-permute-start(f32[2,64,2048]{2,1,0:T(8,128)} %get-tuple-element.14), channel_id=1, source_target_pairs={{0,2},{1,3},{2,4},{3,5},{4,6},{5,7},{6,0},{7,1},{8,10},{9,11},{10,... | collective-permute-start | bytes 3145736 | tf_op jit(solution)/shard_map/ppermute | solution.py:301
  55.8 1.9 %collective-permute-start.1 = (f32[2,64,2048]{2,1,0:T(8,128)}, f32[2,64,2048]{2,1,0:T(8,128)S(1)}, u32[]{:S(2)}, u32[]{:S(2)}) collective-permute-start(f32[2,64,2048]{2,1,0:T(8,128)} %get-tuple-element.15), channel_id=1, source_target_pairs={{0,6},{1,7},{2,0},{3,1},{4,2},{5,3},{6,4},{7,5},{8,14},{9,15},{10,... | collective-permute-start | bytes 3145736 | tf_op jit(solution)/shard_map/ppermute | solution.py:302
  57.8 0.0 copy-start
  57.8 1.6 %copy-done = bf16[4,2,64,2048]{3,2,1,0:T(8,128)(2,1)S(1)} copy-done((bf16[4,2,64,2048]{3,2,1,0:T(8,128)(2,1)S(1)}, bf16[4,2,64,2048]{3,2,1,0:T(8,128)(2,1)}, u32[]{:S(2)}) %copy-start) | copy-done | bytes 2097176
  59.3 0.0 copy-start.1
  59.3 1.6 %copy-done.1 = bf16[4,2,64,2048]{3,2,1,0:T(8,128)(2,1)S(1)} copy-done((bf16[4,2,64,2048]{3,2,1,0:T(8,128)(2,1)S(1)}, bf16[4,2,64,2048]{3,2,1,0:T(8,128)(2,1)}, u32[]{:S(2)}) %copy-start.1) | copy-done | bytes 2097176
  60.9 0.0 copy-start.2
  60.9 1.0 %copy-done.2 = bf16[4,256,256]{2,1,0:T(8,128)(2,1)S(1)} copy-done((bf16[4,256,256]{2,1,0:T(8,128)(2,1)S(1)}, bf16[4,256,256]{2,1,0:T(8,128)(2,1)}, u32[]{:S(2)}) %copy-start.2) | copy-done | bytes 524312
  62.0 0.0 copy-start.3
  62.0 0.7 copy-done.3
  62.7 0.0 copy-start.4
  62.7 12.8 %table_grads.1 = (bf16[2048,2048]{1,0:T(8,128)(2,1)}, bf16[2048,2048]{1,0:T(8,128)(2,1)}) custom-call(s32[8,128]{1,0:T(8,128)S(1)} %copy-done.3, bf16[4,256,256]{2,1,0:T(8,128)(2,1)S(1)} %copy-done.2, bf16[512,2048]{1,0:T(8,128)(2,1)S(1)} %bitcast.9, bf16[512,2048]{1,0:T(8,128)(2,1)S(1)} %bitcast.10), custom_call_target="tpu_custom_call" | custom-call | flops 8589934592 | bytes 20971520 | tf_op jit(solution)/shard_map/table_grads/pallas_call | solution.py:306
  75.5 5.9 %collective-permute-done = f32[2,64,2048]{2,1,0:T(8,128)S(1)} collective-permute-done((f32[2,64,2048]{2,1,0:T(8,128)}, f32[2,64,2048]{2,1,0:T(8,128)S(1)}, u32[]{:S(2)}, u32[]{:S(2)}) %collective-permute-start) | collective-permute-done | bytes 1048608 | tf_op jit(solution)/shard_map/ppermute | solution.py:301
  81.4 0.0 collective-permute-done.1
  81.4 0.0 copy-done.4
  81.4 0.2 add_convert_fusion
  81.6 0.8 slice_bitcast_fusion
Async XLA Ops:
  55.0 26.4 %collective-permute-start = (f32[2,64,2048]{2,1,0:T(8,128)}, f32[2,64,2048]{2,1,0:T(8,128)S(1)}, u32[]{:S(2)}, u32[]{:S(2)}) collective-permute-start(f32[2,64,2048]{2,1,0:T(8,128)} %get-tuple-element.14), channel_id=1, source_target_pairs={{0,2},{1,3},{2,4},{3,5},{4,6},{5,7},{6,0},{7,1},{8,10},{9,11},{10,... | collective-permute-start | bytes 3145736 | tf_op jit(solution)/shard_map/ppermute | solution.py:301
  55.8 25.6 %collective-permute-start.1 = (f32[2,64,2048]{2,1,0:T(8,128)}, f32[2,64,2048]{2,1,0:T(8,128)S(1)}, u32[]{:S(2)}, u32[]{:S(2)}) collective-permute-start(f32[2,64,2048]{2,1,0:T(8,128)} %get-tuple-element.15), channel_id=1, source_target_pairs={{0,6},{1,7},{2,0},{3,1},{4,2},{5,3},{6,4},{7,5},{8,14},{9,15},{10,... | collective-permute-start | bytes 3145736 | tf_op jit(solution)/shard_map/ppermute | solution.py:302
  57.8 1.6 %copy-start = (bf16[4,2,64,2048]{3,2,1,0:T(8,128)(2,1)S(1)}, bf16[4,2,64,2048]{3,2,1,0:T(8,128)(2,1)}, u32[]{:S(2)}) copy-start(bf16[4,2,64,2048]{3,2,1,0:T(8,128)(2,1)} %get-tuple-element.18) | copy-start | bytes 6291460
  59.3 1.6 %copy-start.1 = (bf16[4,2,64,2048]{3,2,1,0:T(8,128)(2,1)S(1)}, bf16[4,2,64,2048]{3,2,1,0:T(8,128)(2,1)}, u32[]{:S(2)}) copy-start(bf16[4,2,64,2048]{3,2,1,0:T(8,128)(2,1)} %get-tuple-element.19) | copy-start | bytes 6291460
  60.9 1.0 %copy-start.2 = (bf16[4,256,256]{2,1,0:T(8,128)(2,1)S(1)}, bf16[4,256,256]{2,1,0:T(8,128)(2,1)}, u32[]{:S(2)}) copy-start(bf16[4,256,256]{2,1,0:T(8,128)(2,1)} %get-tuple-element.17.wc_ref) | copy-start | bytes 1572868
  62.0 0.7 copy-start.3
  62.7 18.7 %copy-start.4 = (f32[2,64,2048]{2,1,0:T(8,128)S(1)}, f32[2,64,2048]{2,1,0:T(8,128)}, u32[]{:S(2)}) copy-start(f32[2,64,2048]{2,1,0:T(8,128)} %get-tuple-element.13) | copy-start | bytes 3145732

commit v2 on v1

v2 whole, which is shorter than its diff:
```python
import functools
import math

import jax
import jax.numpy as jnp
from jax import lax
from jax.experimental import pallas as pl
from jax.experimental.pallas import tpu as pltpu
from jax.sharding import PartitionSpec as P

MESH = pl.DeviceIdType.MESH
F32 = jnp.float32
BF16 = jnp.bfloat16
NT = (((1,), (1,)), ((), ()))
OWN, RIGHT, FAR, LEFT = 0, 1, 2, 3
ORDER = (RIGHT, LEFT, FAR, OWN)
COLS = 512
WIDE = 1024
LATE = 256


def gelu_pair(pre_act):
    normal_cdf = 0.5 * (1.0 + lax.erf(pre_act * (2.0 ** -0.5)))
    normal_pdf = jnp.exp(-0.5 * pre_act * pre_act) * ((2.0 * math.pi) ** -0.5)
    return pre_act * normal_cdf, normal_cdf + pre_act * normal_pdf


def exchange_kernel(x_hbm, dy_hbm, slot_hbm, gate_hbm, req_hbm, u_hbm, v_hbm,
                    y_next, dx_next, own_out, xall_out, dyall_out, ct_out, wt_out,
                    u_v, v_v, ureq, vreq, onehot, xa, da, gall, qall, slot_in, gate_in, slots, gates, gmix, gloc, wc, ct, wt, part, sib, near, far,
                    load_sem, out_sem, q_send, q_recv, g_send, g_recv, ax_send, ax_recv, d2d_send, d2d_recv,
                    p_send, p_recv, n_send, n_recv, f_send, f_recv):
    n_dev, n_req = req_hbm.shape
    n_chip = n_dev // 2
    n_tok, width = x_hbm.shape
    n_rows = u_v.shape[0]
    shift = n_req.bit_length() - 1
    me = lax.axis_index('ep')
    core = lax.rem(me, 2)
    chip = me // 2
    other = 1 - core

    def dev(rel, which):
        return lax.rem(chip + rel, n_chip) * 2 + which

    right, left, mate = dev(RIGHT, core), dev(LEFT, core), dev(OWN, other)
    peers = [(rel, flip) for rel in range(4) for flip in range(2) if (rel, flip) != (0, 0)]

    def peer_core(flip):
        return core if flip == 0 else other

    barrier = pltpu.get_barrier_semaphore()
    for rel, flip in peers:
        pl.semaphore_signal(barrier, inc=1, device_id={'ep': dev(rel, peer_core(flip))}, device_id_type=MESH)

    load_x = pltpu.make_async_copy(x_hbm, xa.at[OWN, core], load_sem.at[0])
    load_d = pltpu.make_async_copy(dy_hbm, da.at[OWN, core], load_sem.at[1])
    load_q = pltpu.make_async_copy(req_hbm, qall.at[OWN, core], load_sem.at[2])
    load_s = pltpu.make_async_copy(slot_hbm, slot_in, load_sem.at[3])
    load_g = pltpu.make_async_copy(gate_hbm, gate_in, load_sem.at[4])
    load_u = pltpu.make_async_copy(u_hbm, u_v, load_sem.at[5])
    load_v = pltpu.make_async_copy(v_hbm, v_v, load_sem.at[6])
    for load in (load_q, load_x, load_d, load_s, load_g, load_u, load_v):
        load.start()

    def rcopy(src, dst, s_sem, r_sem, target):
        return pltpu.make_async_remote_copy(src_ref=src, dst_ref=dst, send_sem=s_sem, recv_sem=r_sem, device_id={'ep': target}, device_id_type=MESH)

    q_copies, g_copies = {}, {}
    for n, (rel, flip) in enumerate(peers):
        back = (4 - rel) % 4
        target = dev(rel, peer_core(flip))
        q_copies[rel, flip] = rcopy(qall.at[OWN, core], qall.at[back, core], q_send.at[n], q_recv.at[n], target)
        g_copies[rel, flip] = rcopy(gloc.at[target], gall.at[back, core], g_send.at[n], g_recv.at[n], target)
    x_right = rcopy(xa.at[OWN, core], xa.at[LEFT, core], ax_send.at[0], ax_recv.at[0], right)
    d_left = rcopy(da.at[OWN, core], da.at[RIGHT, core], ax_send.at[1], ax_recv.at[1], left)
    d_right = rcopy(da.at[OWN, core], da.at[LEFT, core], ax_send.at[2], ax_recv.at[2], right)
    x_left = rcopy(xa.at[OWN, core], xa.at[RIGHT, core], ax_send.at[3], ax_recv.at[3], left)
    x_far = rcopy(xa.at[LEFT, core], xa.at[FAR, core], ax_send.at[4], ax_recv.at[4], right)
    d_far = rcopy(da.at[RIGHT, core], da.at[FAR, core], ax_send.at[5], ax_recv.at[5], left)
    x_mate = [rcopy(xa.at[rel, core], xa.at[rel, core], d2d_send.at[rel, 0], d2d_recv.at[rel, 0], mate) for rel in range(4)]
    d_mate = [rcopy(da.at[rel, core], da.at[rel, core], d2d_send.at[rel, 1], d2d_recv.at[rel, 1], mate) for rel in range(4)]

    load_q.wait()
    load_x.wait()
    load_d.wait()
    pl.semaphore_wait(barrier, len(peers))
    near_peers = [key for key in peers if key[0] != FAR]
    far_peers = [key for key in peers if key[0] == FAR]
    for key in near_peers:
        q_copies[key].start()
    x_right.start()
    d_left.start()
    for key in far_peers:
        q_copies[key].start()
    d_right.start()
    x_left.start()
    x_mate[OWN].start()
    d_mate[OWN].start()
    load_s.wait()
    load_g.wait()
    slots[...] = jnp.transpose(slot_in[...].astype(F32)).astype(jnp.int32)
    gates[...] = jnp.transpose(gate_in[...])

    own_iota = lax.broadcasted_iota(jnp.int32, (n_dev, n_req), 0)
    sub_iota = lax.broadcasted_iota(jnp.int32, (n_req, n_req), 0)

    def gate_step(step, carry):
        base = pl.multiple_of(step * 8, 8)
        s_blk = slots[pl.ds(base, 8), :]
        g_blk = gates[pl.ds(base, 8), :]
        for j in range(8):
            s_row = s_blk[j:j + 1, :]
            g_row = g_blk[j:j + 1, :]
            spread = jnp.where(own_iota == (s_row >> shift), g_row, 0.0)
            hi = spread.astype(BF16).astype(F32)
            rest = spread - hi
            mid = rest.astype(BF16).astype(F32)
            lo = rest - mid
            lhs = jnp.concatenate([hi, mid, lo], axis=0).astype(BF16)
            hot = jnp.where(sub_iota == (s_row & (n_req - 1)), 1.0, 0.0).astype(BF16)
            res = lax.dot_general(lhs, hot, NT, preferred_element_type=F32)
            start = pl.multiple_of((base + j) * n_dev, n_dev)
            gmix[pl.ds(start, n_dev), :] = res[0:n_dev] + res[n_dev:2 * n_dev] + res[2 * n_dev:3 * n_dev]
        return carry

    lax.fori_loop(0, n_tok // 8, gate_step, 0)
    for o in range(n_dev):
        gloc[o] = gmix[pl.ds(o, n_tok, stride=n_dev), :]
    for key in near_peers + far_peers:
        g_copies[key].start()
    gall[OWN, core] = gloc[me]

    lane_iota = lax.broadcasted_iota(jnp.int32, (n_req, n_req), 1).astype(F32)

    def lists(rel):
        return [qall[rel, which, pl.ds(me, 1), :] for which in range(2)]

    def gather_hot(rels):
        rows = [r.astype(F32) for rel in rels for r in lists(rel)]
        stack = jnp.broadcast_to(rows[0], (n_req, n_req))
        for n in range(1, len(rows)):
            stack = jnp.where(sub_iota == n, rows[n], stack)
        cols = jnp.transpose(stack)
        for n in range(len(rows)):
            col = jnp.broadcast_to(cols[:, n:n + 1], (n_req, n_req))
            for blk in range(n_rows // n_req):
                onehot[pl.ds(n * n_req, n_req), pl.ds(blk * n_req, n_req)] = jnp.where(col - blk * n_req == lane_iota, 1.0, 0.0).astype(BF16)

    def gather_rows(rels, src, dst, first, last):
        size = len(rels) * 2 * n_req
        base = ORDER.index(rels[0]) * 2 * n_req

        def body(step, carry):
            cols = pl.ds(pl.multiple_of(step * WIDE, WIDE), WIDE)
            dst[base:base + size, cols] = jnp.dot(onehot[0:size, :], src[:, cols], preferred_element_type=F32).astype(BF16)
            return carry

        lax.fori_loop(first, last, body, 0)

    def rows_of(table, rel, cols=slice(None)):
        base = ORDER.index(rel) * 2 * n_req
        return table[base:base + 2 * n_req, cols]

    zeros = jnp.zeros((n_tok, n_req), BF16)

    def scores(rel):
        pre = lax.dot_general(xa[rel].reshape(2 * n_tok, width), rows_of(ureq, rel), NT, preferred_element_type=F32)
        back_dot = lax.dot_general(da[rel].reshape(2 * n_tok, width), rows_of(vreq, rel), NT, preferred_element_type=F32)
        for flip in range(2):
            if (rel, flip) != (0, 0):
                g_copies[(4 - rel) % 4, flip].wait_recv()
        for which in range(2):
            t_lo, s_lo = which * n_tok, which * n_req
            act, slope = gelu_pair(pre[t_lo:t_lo + n_tok, s_lo:s_lo + n_req])
            gate = gall[rel, which]
            z_lo = (1 - which) * n_req
            wc[rel, pl.ds(t_lo, n_tok), pl.ds(s_lo, n_req)] = (gate * act).astype(BF16)
            wc[rel, pl.ds(t_lo, n_tok), pl.ds(z_lo, n_req)] = zeros
            wc[rel, pl.ds(2 * n_tok + t_lo, n_tok), pl.ds(s_lo, n_req)] = (gate * slope * back_dot[t_lo:t_lo + n_tok, s_lo:s_lo + n_req]).astype(BF16)
            wc[rel, pl.ds(2 * n_tok + t_lo, n_tok), pl.ds(z_lo, n_req)] = zeros

    theirs = pl.ds(pl.multiple_of(other * n_tok, n_tok), n_tok)
    mine = pl.ds(pl.multiple_of(core * n_tok, n_tok), n_tok)

    def partial(rel, out):
        table = vreq if out == 0 else ureq

        def body(step, carry):
            cols = pl.ds(pl.multiple_of(step * COLS, COLS), COLS)
            part[rel, out, :, cols] = jnp.dot(wc[rel, out * 2 * n_tok:(out + 1) * 2 * n_tok, :], rows_of(table, rel, cols), preferred_element_type=F32)
            return carry

        lax.fori_loop(0, width // COLS, body, 0)
        send = rcopy(part.at[rel, out, theirs, :], sib.at[rel, out], p_send.at[rel, out], p_recv.at[rel, out], mate)
        send.start()
        return send

    def add_mate(rel, out, send):
        send.wait_recv()
        sib[rel, out] = sib[rel, out] + part[rel, out, mine, :]

    def place(rel):
        rows = jnp.concatenate(lists(rel), axis=1)
        blk = n_rows // 2

        def body(step, carry):
            base = pl.multiple_of(step * blk, blk)
            hot = jnp.where(lax.broadcasted_iota(jnp.int32, (blk, 2 * n_req), 0) + base == rows, 1.0, 0.0).astype(BF16)
            coef = lax.dot_general(hot, wc[rel], NT, preferred_element_type=F32).astype(BF16)
            wt[pl.ds(base, blk), rel * 2 * n_tok:(rel + 1) * 2 * n_tok] = coef[:, :2 * n_tok]
            ct[pl.ds(base, blk), rel * 2 * n_tok:(rel + 1) * 2 * n_tok] = coef[:, 2 * n_tok:]
            return carry

        lax.fori_loop(0, n_rows // blk, body, 0)

    def need(rel):
        x_mate[rel].wait_recv()
        d_mate[rel].wait_recv()

    n_wide = width // WIDE
    cut = width - LATE
    for rel, flip in near_peers:
        q_copies[rel, flip].wait_recv()
    gather_hot((RIGHT, LEFT))
    load_u.wait()
    gather_rows((RIGHT, LEFT), u_v, ureq, 0, n_wide)
    x_right.wait_recv()
    x_far.start()
    x_mate[LEFT].start()
    d_left.wait_recv()
    d_far.start()
    d_mate[RIGHT].start()
    load_v.wait()
    gather_rows((RIGHT, LEFT), v_v, vreq, 0, n_wide)
    for rel, flip in far_peers:
        q_copies[rel, flip].wait_recv()
    gather_hot((FAR,))
    gather_rows((FAR,), u_v, ureq, 0, 1)
    d_right.wait_recv()
    d_mate[LEFT].start()
    x_left.wait_recv()
    x_mate[RIGHT].start()
    gather_rows((FAR,), u_v, ureq, 1, n_wide)
    need(RIGHT)
    scores(RIGHT)
    s_right_d = partial(RIGHT, 1)
    need(LEFT)
    scores(LEFT)
    s_left_y = partial(LEFT, 0)
    add_mate(RIGHT, 1, s_right_d)
    n_right = rcopy(sib.at[RIGHT, 1, :, 0:cut], near.at[1], n_send.at[1], n_recv.at[1], right)
    n_right.start()
    add_mate(LEFT, 0, s_left_y)
    n_left = rcopy(sib.at[LEFT, 0, :, 0:cut], near.at[0], n_send.at[0], n_recv.at[0], left)
    n_left.start()
    gather_rows((FAR,), v_v, vreq, 0, n_wide)
    x_far.wait_recv()
    x_mate[FAR].start()
    d_far.wait_recv()
    d_mate[FAR].start()
    s_right_y = partial(RIGHT, 0)
    s_left_d = partial(LEFT, 1)
    need(FAR)
    scores(FAR)
    s_far = [partial(FAR, 0), partial(FAR, 1)]
    add_mate(FAR, 0, s_far[0])
    f_y = rcopy(sib.at[FAR, 0], far.at[0], f_send.at[0], f_recv.at[0], right)
    f_y.start()
    add_mate(FAR, 1, s_far[1])
    f_d = rcopy(sib.at[FAR, 1], far.at[1], f_send.at[1], f_recv.at[1], left)
    f_d.start()
    gather_hot((OWN,))
    gather_rows((OWN,), u_v, ureq, 0, n_wide)
    gather_rows((OWN,), v_v, vreq, 0, n_wide)
    need(OWN)
    scores(OWN)
    s_own = [partial(OWN, 0), partial(OWN, 1)]
    o_x = pltpu.make_async_copy(xa, xall_out, out_sem.at[0])
    o_d = pltpu.make_async_copy(da, dyall_out, out_sem.at[1])
    o_x.start()
    o_d.start()
    for rel in range(4):
        place(rel)
    o_c = pltpu.make_async_copy(ct, ct_out, out_sem.at[2])
    o_w = pltpu.make_async_copy(wt, wt_out, out_sem.at[3])
    o_c.start()
    o_w.start()
    add_mate(RIGHT, 0, s_right_y)
    add_mate(LEFT, 1, s_left_d)
    add_mate(OWN, 0, s_own[0])
    add_mate(OWN, 1, s_own[1])
    n_left.wait_recv()
    sib[OWN, 0, :, 0:cut] = sib[OWN, 0, :, 0:cut] + near[0]
    n_right.wait_recv()
    sib[OWN, 1, :, 0:cut] = sib[OWN, 1, :, 0:cut] + near[1]
    o_own = pltpu.make_async_copy(sib.at[OWN], own_out, out_sem.at[4])
    o_own.start()
    o_rest = [pltpu.make_async_copy(sib.at[RIGHT, 1, :, cut:width], y_next.at[:, width:width + LATE], out_sem.at[7]),
              pltpu.make_async_copy(sib.at[LEFT, 0, :, cut:width], dx_next.at[:, width:width + LATE], out_sem.at[8])]
    for copy in o_rest:
        copy.start()
    for key in q_copies:
        q_copies[key].wait_send()
        g_copies[key].wait_send()
    for copy in (x_right, d_left, d_right, x_left, x_far, d_far, *x_mate, *d_mate, *s_far, s_right_d, s_right_y, s_left_y, s_left_d, *s_own, n_left, n_right):
        copy.wait_send()
    for copy in (o_x, o_d, o_c, o_w, o_own, *o_rest):
        copy.wait()
    f_y.wait_recv()
    sib[RIGHT, 0] = sib[RIGHT, 0] + far[0]
    o_y = pltpu.make_async_copy(sib.at[RIGHT, 0], y_next.at[:, 0:width], out_sem.at[5])
    o_y.start()
    f_d.wait_recv()
    sib[LEFT, 1] = sib[LEFT, 1] + far[1]
    o_dx = pltpu.make_async_copy(sib.at[LEFT, 1], dx_next.at[:, 0:width], out_sem.at[6])
    o_dx.start()
    f_y.wait_send()
    f_d.wait_send()
    o_y.wait()
    o_dx.wait()


def grad_kernel(ct_ref, wt_ref, xall_ref, dyall_ref, gu_ref, gv_ref):
    width = gu_ref.shape[1]
    for step in range(width // WIDE):
        cols = pl.ds(step * WIDE, WIDE)
        gu_ref[:, cols] = jnp.dot(ct_ref[...], xall_ref[:, cols], preferred_element_type=F32).astype(BF16)
        gv_ref[:, cols] = jnp.dot(wt_ref[...], dyall_ref[:, cols], preferred_element_type=F32).astype(BF16)


def solution(mesh):
    n_dev = mesh.shape['ep']
    tok_spec = P(('dp', 'ep'))
    table_spec = P('ep')
    hbm = pl.BlockSpec(memory_space=pl.ANY)
    dma = pltpu.SemaphoreType.DMA
    sds = jax.ShapeDtypeStruct

    def per_device(tokens, slot_ids, request_rows, gate_vals, grad_out, up_local, down_local):
        n_tok, width = tokens.shape
        n_rows = up_local.shape[0]
        n_req = request_rows.shape[2]
        sel = slot_ids.shape[1] * slot_ids.shape[2]
        n_all = n_dev * n_tok
        y_next, dx_next, own, xall, dyall, ct, wt = pl.pallas_call(
            exchange_kernel,
            name='exchange',
            out_shape=(sds((n_tok, width + LATE), F32), sds((n_tok, width + LATE), F32), sds((2, n_tok, width), F32),
                       sds((4, 2, n_tok, width), BF16), sds((4, 2, n_tok, width), BF16), sds((n_rows, n_all), BF16), sds((n_rows, n_all), BF16)),
            in_specs=[hbm] * 7,
            out_specs=(hbm,) * 7,
            scratch_shapes=[
                pltpu.VMEM((n_rows, width), BF16), pltpu.VMEM((n_rows, width), BF16),
                pltpu.VMEM((n_dev * n_req, width), BF16), pltpu.VMEM((n_dev * n_req, width), BF16),
                pltpu.VMEM((4 * n_req, n_rows), BF16),
                pltpu.VMEM((4, 2, n_tok, width), BF16), pltpu.VMEM((4, 2, n_tok, width), BF16),
                pltpu.VMEM((4, 2, n_tok, n_req), F32), pltpu.VMEM((4, 2, n_dev, n_req), jnp.int32),
                pltpu.VMEM((sel, n_tok), jnp.int32), pltpu.VMEM((sel, n_tok), F32), pltpu.VMEM((n_tok, sel), jnp.int32), pltpu.VMEM((n_tok, sel), F32),
                pltpu.VMEM((n_tok * n_dev, n_req), F32), pltpu.VMEM((n_dev, n_tok, n_req), F32),
                pltpu.VMEM((4, 4 * n_tok, 2 * n_req), BF16), pltpu.VMEM((n_rows, n_all), BF16), pltpu.VMEM((n_rows, n_all), BF16),
                pltpu.VMEM((4, 2, 2 * n_tok, width), F32), pltpu.VMEM((4, 2, n_tok, width), F32),
                pltpu.VMEM((2, n_tok, width - LATE), F32), pltpu.VMEM((2, n_tok, width), F32),
                dma((7,)), dma((9,)), dma((7,)), dma((7,)), dma((7,)), dma((7,)), dma((6,)), dma((6,)), dma((4, 2)), dma((4, 2)),
                dma((4, 2)), dma((4, 2)), dma((2,)), dma((2,)), dma((2,)), dma((2,)),
            ],
            compiler_params=pltpu.CompilerParams(collective_id=0, has_side_effects=True, vmem_limit_bytes=60 * 2 ** 20),
            cost_estimate=pl.CostEstimate(flops=4 * n_dev * n_req * n_rows * width, bytes_accessed=6 * n_rows * width, transcendentals=0),
        )(tokens, grad_out, slot_ids.reshape(n_tok, sel).T, gate_vals.reshape(n_tok, sel).T, request_rows[0], up_local, down_local)

        up_chip = [(d, (d + 2) % n_dev) for d in range(n_dev)]
        down_chip = [(d, (d - 2) % n_dev) for d in range(n_dev)]
        y_last = lax.ppermute(y_next, 'ep', up_chip)
        dx_last = lax.ppermute(dx_next, 'ep', down_chip)

        blk = min(512, n_rows)
        row_spec = lambda cols: pl.BlockSpec((blk, cols), lambda i: (i, 0))
        full_spec = pl.BlockSpec((n_all, width), lambda i: (0, 0))
        grad_up, grad_down = pl.pallas_call(
            grad_kernel,
            name='table_grads',
            out_shape=(sds((n_rows, width), BF16),) * 2,
            grid=(n_rows // blk,),
            in_specs=[row_spec(n_all), row_spec(n_all), full_spec, full_spec],
            out_specs=(row_spec(width),) * 2,
            compiler_params=pltpu.CompilerParams(vmem_limit_bytes=60 * 2 ** 20),
            cost_estimate=pl.CostEstimate(flops=4 * n_rows * n_all * width, bytes_accessed=4 * (n_rows + n_all) * width, transcendentals=0),
        )(ct, wt, xall.reshape(n_all, width), dyall.reshape(n_all, width))
        rest = lambda a: jnp.pad(a[:, width:], ((0, 0), (width - LATE, 0)))
        y = own[0] + y_last[:, :width] + rest(dx_last)
        dx = own[1] + dx_last[:, :width] + rest(y_last)
        return y.astype(BF16), dx.astype(BF16), grad_up, grad_down

    return jax.shard_map(per_device, mesh=mesh, in_specs=(tok_spec, tok_spec, tok_spec, tok_spec, tok_spec, table_spec, table_spec), out_specs=(tok_spec, tok_spec, tok_spec, tok_spec), check_vma=False)
```

time: 82.7 us -> 67.8 us (0.82)
  local copies, waits for them, and re-layouts: 8.81 us -> 0.02 us
  waiting for transfers between devices: 5.88 us -> 0.01 us
    ppermute x2, waiting for transfers between devices: 5.88 us -> 0.01 us  [the longest x1 0.01 us: per_device(): dx_last = lax.ppermute(dx_next, 'ep', down_chip)]
    unnamed x10 -> x2, local copies, waits for them, and re-layouts: 4.91 us -> 0.01 us
    reshape x2 -> x0, local copies, waits for them, and re-layouts: 3.07 us -> none  [the longest x1 1.54 us: per_device(): slot_ids.reshape(n_tok, sel)]
    pallas_call x1, Pallas kernels: 51.3 us -> 49.8 us  [per_device(): pl.pallas_call(exchange_kernel, name='exchange', out_shape=(sds((n_tok, w...]
  transfers between devices with their start and end apart: 2 -> 2, of which waited for: 1 -> 0; matrix products, arithmetic and copies ran while one was open for 0% -> 0% of each run, Pallas kernels for 16% -> 20%
where the time goes in v2:
time: 67.8 us
  Pallas kernels  63.4 us (94%)
  starting transfers between devices  2.76 us (4%)
  other arithmetic  0.9 us (1%)
  between operations  0.68 us (1%)
    pallas_call x1, Pallas kernels, per_device(): pl.pallas_call(exchange_kernel, name='exchange', out_shape=(sds((n_tok, w...  49.8 us
    pallas_call x1, Pallas kernels, per_device(): pl.pallas_call(grad_kernel, name='table_grads', out_shape=(sds((n_rows, w...  13.6 us
    ppermute x1, starting transfers between devices, per_device(): dx_last = lax.ppermute(dx_next, 'ep', down_chip)  2.65 us
  transfers between devices with their start and end apart: 2, of which 0 were waited for; matrix products, arithmetic and copies ran while one was open for 0% of the time, Pallas kernels for 20%

profile of v2, /device:TPU:81, one launch (start us, length us, event | category | flops | bytes accessed | tf_op | source)
XLA Modules:
  0.0 67.8 jit_solution(12241398967792072307)
XLA Ops:
  0.6 49.8 %exchange.1 = (f32[64,2304]{1,0:T(8,128)}, f32[64,2304]{1,0:T(8,128)}, f32[2,64,2048]{2,1,0:T(8,128)}, bf16[4,2,64,2048]{3,2,1,0:T(8,128)(2,1)}, bf16[4,2,64,204...) custom-call(bf16[64,2048]{1,0:T(8,128)(2,1)} %x_hbm.1, bf16[64,2048]{1,0:T(8,128)(2,1)} %dy_hbm.1, ...), custom_call_target="tpu_custom_call" | custom-call | flops 17179869184 | bytes 25165824 | tf_op jit(solution)/shard_map/exchange/pallas_call | solution.py:346
  50.5 0.1 collective-permute-start
  50.6 2.7 %collective-permute-start.1 = (f32[64,2304]{1,0:T(8,128)}, f32[64,2304]{1,0:T(8,128)S(1)}, u32[]{:S(2)}, u32[]{:S(2)}) collective-permute-start(f32[64,2304]{1,0:T(8,128)} %get-tuple-element.15), channel_id=1, source_target_pairs={{0,6},{1,7},{2,0},{3,1},{4,2},{5,3},{6,4},{7,5},{8,14},{9,15},{10,... | collective-permute-start | bytes 1769480 | tf_op jit(solution)/shard_map/ppermute | solution.py:374
  53.2 0.0 copy-start
  53.2 13.6 %table_grads.1 = (bf16[2048,2048]{1,0:T(8,128)(2,1)}, bf16[2048,2048]{1,0:T(8,128)(2,1)}) custom-call(bf16[2048,512]{1,0:T(8,128)(2,1)} %get-tuple-element.16.ct_ref, bf16[2048,512]{1,0:T(8,128)(2,1)} %get-tuple-element.17.wt_ref, bf16[512,2048]{1,0:T(8,128)(2,1)} %bitcast.16, bf16[512,2048]{1,0:T(8,128)(2,1)} %bitcast.17), custom_call_target="tpu_custom_call" | custom-call | flops 8589934592 | bytes 20971520 | tf_op jit(solution)/shard_map/table_grads/pallas_call | solution.py:379
  66.8 0.0 collective-permute-done
  66.8 0.0 collective-permute-done.1
  66.8 0.0 copy-done
  66.9 0.9 %fusion.1 = (bf16[64,2048]{1,0:T(8,128)(2,1)}, bf16[64,2048]{1,0:T(8,128)(2,1)}) fusion(f32[64,2304]{1,0:T(8,128)S(1)} %collective-permute-done.1, f32[64,256]{1,0:T(8,128)S(1)} %slice.27, f32[2,64,2048]{2,1,0:T(8,128)S(1)} %copy-done, f32[64,256]{1,0:T(8,128)S(1)} %slice.25, f32[64,2304]{1,0:T(8,128)S(1)} %collective-permute-done), kind=kLoop, calls=%fused_computation.2 | loop fusion | flops 786432 | bytes 2752512 | tf_op jit(solution)/shard_map/convert_element_type | solution.py:392
  (2 shorter events, 0.0 us)
Async XLA Ops:
  50.5 16.4 %collective-permute-start = (f32[64,2304]{1,0:T(8,128)}, f32[64,2304]{1,0:T(8,128)S(1)}, u32[]{:S(2)}, u32[]{:S(2)}) collective-permute-start(f32[64,2304]{1,0:T(8,128)} %get-tuple-element.14), channel_id=1, source_target_pairs={{0,2},{1,3},{2,4},{3,5},{4,6},{5,7},{6,0},{7,1},{8,10},{9,11},{10,... | collective-permute-start | bytes 1769480 | tf_op jit(solution)/shard_map/ppermute | solution.py:373
  50.6 16.3 %collective-permute-start.1 = (f32[64,2304]{1,0:T(8,128)}, f32[64,2304]{1,0:T(8,128)S(1)}, u32[]{:S(2)}, u32[]{:S(2)}) collective-permute-start(f32[64,2304]{1,0:T(8,128)} %get-tuple-element.15), channel_id=1, source_target_pairs={{0,6},{1,7},{2,0},{3,1},{4,2},{5,3},{6,4},{7,5},{8,14},{9,15},{10,... | collective-permute-start | bytes 1769480 | tf_op jit(solution)/shard_map/ppermute | solution.py:374
  53.2 13.6 %copy-start = (f32[2,64,2048]{2,1,0:T(8,128)S(1)}, f32[2,64,2048]{2,1,0:T(8,128)}, u32[]{:S(2)}) copy-start(f32[2,64,2048]{2,1,0:T(8,128)} %get-tuple-element.13) | copy-start | bytes 3145732

commit v3 on v2

--- a/solution.py
+++ b/solution.py
@@ -16,7 +16,8 @@
 ORDER = (RIGHT, LEFT, FAR, OWN)
 COLS = 512
 WIDE = 1024
-LATE = 256
+LATE = 512
+HALVES = 2
 
 
 def gelu_pair(pre_act):
@@ -27,7 +28,7 @@
 
 def exchange_kernel(x_hbm, dy_hbm, slot_hbm, gate_hbm, req_hbm, u_hbm, v_hbm,
                     y_next, dx_next, own_out, xall_out, dyall_out, ct_out, wt_out,
-                    u_v, v_v, ureq, vreq, onehot, xa, da, gall, qall, slot_in, gate_in, slots, gates, gmix, gloc, wc, ct, wt, part, sib, near, far,
+                    u_v, v_v, ureq, vreq, onehot, xa, da, gall, qall, gpass, slot_in, gate_in, slots, gates, gmix, gloc, dots_x, dots_d, wc, ct, wt, part, sib, near, far,
                     load_sem, out_sem, q_send, q_recv, g_send, g_recv, ax_send, ax_recv, d2d_send, d2d_recv,
                     p_send, p_recv, n_send, n_recv, f_send, f_recv):
     n_dev, n_req = req_hbm.shape
@@ -44,7 +45,7 @@
         return lax.rem(chip + rel, n_chip) * 2 + which
 
     right, left, mate = dev(RIGHT, core), dev(LEFT, core), dev(OWN, other)
-    peers = [(rel, flip) for rel in range(4) for flip in range(2) if (rel, flip) != (0, 0)]
+    peers = [(rel, flip) for rel in (OWN, RIGHT, LEFT) for flip in range(2) if (rel, flip) != (OWN, 0)]
 
     def peer_core(flip):
         return core if flip == 0 else other
@@ -72,6 +73,9 @@
         target = dev(rel, peer_core(flip))
         q_copies[rel, flip] = rcopy(qall.at[OWN, core], qall.at[back, core], q_send.at[n], q_recv.at[n], target)
         g_copies[rel, flip] = rcopy(gloc.at[target], gall.at[back, core], g_send.at[n], g_recv.at[n], target)
+    q_pass = [rcopy(qall.at[LEFT, core], qall.at[FAR, core], q_send.at[5 + flip], q_recv.at[5 + flip], dev(RIGHT, peer_core(flip))) for flip in range(2)]
+    g_out = [rcopy(gloc.at[dev(FAR, peer_core(flip))], gpass.at[flip], g_send.at[5 + flip], g_recv.at[5 + flip], (right, left)[flip]) for flip in range(2)]
+    g_pass = [rcopy(gpass.at[flip], gall.at[FAR, core], g_send.at[7 + flip], g_recv.at[7 + flip], dev((RIGHT, LEFT)[flip], peer_core(flip))) for flip in range(2)]
     x_right = rcopy(xa.at[OWN, core], xa.at[LEFT, core], ax_send.at[0], ax_recv.at[0], right)
     d_left = rcopy(da.at[OWN, core], da.at[RIGHT, core], ax_send.at[1], ax_recv.at[1], left)
     d_right = rcopy(da.at[OWN, core], da.at[LEFT, core], ax_send.at[2], ax_recv.at[2], right)
@@ -85,16 +89,10 @@
     load_x.wait()
     load_d.wait()
     pl.semaphore_wait(barrier, len(peers))
-    near_peers = [key for key in peers if key[0] != FAR]
-    far_peers = [key for key in peers if key[0] == FAR]
-    for key in near_peers:
+    for key in peers:
         q_copies[key].start()
     x_right.start()
     d_left.start()
-    for key in far_peers:
-        q_copies[key].start()
-    d_right.start()
-    x_left.start()
     x_mate[OWN].start()
     d_mate[OWN].start()
     load_s.wait()
@@ -127,7 +125,15 @@
     lax.fori_loop(0, n_tok // 8, gate_step, 0)
     for o in range(n_dev):
         gloc[o] = gmix[pl.ds(o, n_tok, stride=n_dev), :]
-    for key in near_peers + far_peers:
+    for key in peers:
+        q_copies[key].wait_recv()
+    for copy in q_pass:
+        copy.start()
+    d_right.start()
+    x_left.start()
+    for copy in g_out:
+        copy.start()
+    for key in peers:
         g_copies[key].start()
     gall[OWN, core] = gloc[me]
 
@@ -164,41 +170,50 @@
 
     zeros = jnp.zeros((n_tok, n_req), BF16)
 
-    def scores(rel):
-        pre = lax.dot_general(xa[rel].reshape(2 * n_tok, width), rows_of(ureq, rel), NT, preferred_element_type=F32)
-        back_dot = lax.dot_general(da[rel].reshape(2 * n_tok, width), rows_of(vreq, rel), NT, preferred_element_type=F32)
+    def tokens_of(buf, rel):
+        return buf[rel].reshape(2 * n_tok, width)
+
+    def dot_x(rel):
+        dots_x[rel] = lax.dot_general(tokens_of(xa, rel), rows_of(ureq, rel), NT, preferred_element_type=F32)
+
+    def dot_d(rel):
+        dots_d[rel] = lax.dot_general(tokens_of(da, rel), rows_of(vreq, rel), NT, preferred_element_type=F32)
+
+    def gates_here(rel):
         for flip in range(2):
-            if (rel, flip) != (0, 0):
+            if rel == FAR:
+                g_pass[flip].wait_recv()
+            elif (rel, flip) != (OWN, 0):
                 g_copies[(4 - rel) % 4, flip].wait_recv()
+
+    def coef(rel, out):
         for which in range(2):
-            t_lo, s_lo = which * n_tok, which * n_req
-            act, slope = gelu_pair(pre[t_lo:t_lo + n_tok, s_lo:s_lo + n_req])
-            gate = gall[rel, which]
-            z_lo = (1 - which) * n_req
-            wc[rel, pl.ds(t_lo, n_tok), pl.ds(s_lo, n_req)] = (gate * act).astype(BF16)
-            wc[rel, pl.ds(t_lo, n_tok), pl.ds(z_lo, n_req)] = zeros
-            wc[rel, pl.ds(2 * n_tok + t_lo, n_tok), pl.ds(s_lo, n_req)] = (gate * slope * back_dot[t_lo:t_lo + n_tok, s_lo:s_lo + n_req]).astype(BF16)
-            wc[rel, pl.ds(2 * n_tok + t_lo, n_tok), pl.ds(z_lo, n_req)] = zeros
+            toks, slot = pl.ds(which * n_tok, n_tok), pl.ds(which * n_req, n_req)
+            act, slope = gelu_pair(dots_x[rel, toks, slot])
+            value = gall[rel, which] * (act if out == 0 else slope)
+            if out == 1:
+                value = value * dots_d[rel, toks, slot]
+            row = pl.ds((out * 2 + which) * n_tok, n_tok)
+            wc[rel, row, slot] = value.astype(BF16)
+            wc[rel, row, pl.ds((1 - which) * n_req, n_req)] = zeros
 
     theirs = pl.ds(pl.multiple_of(other * n_tok, n_tok), n_tok)
     mine = pl.ds(pl.multiple_of(core * n_tok, n_tok), n_tok)
 
+    span = [pl.ds(h * width // HALVES, width // HALVES) for h in range(HALVES)]
+
     def partial(rel, out):
         table = vreq if out == 0 else ureq
-
-        def body(step, carry):
-            cols = pl.ds(pl.multiple_of(step * COLS, COLS), COLS)
+        sends = []
+        for h, cols in enumerate(span):
             part[rel, out, :, cols] = jnp.dot(wc[rel, out * 2 * n_tok:(out + 1) * 2 * n_tok, :], rows_of(table, rel, cols), preferred_element_type=F32)
-            return carry
-
-        lax.fori_loop(0, width // COLS, body, 0)
-        send = rcopy(part.at[rel, out, theirs, :], sib.at[rel, out], p_send.at[rel, out], p_recv.at[rel, out], mate)
-        send.start()
-        return send
-
-    def add_mate(rel, out, send):
-        send.wait_recv()
-        sib[rel, out] = sib[rel, out] + part[rel, out, mine, :]
+            sends.append(rcopy(part.at[rel, out, theirs, cols], sib.at[rel, out, :, cols], p_send.at[rel, out, h], p_recv.at[rel, out, h], mate))
+            sends[-1].start()
+        return sends
+
+    def add_mate(rel, out, sends, h):
+        sends[h].wait_recv()
+        sib[rel, out, :, span[h]] = sib[rel, out, :, span[h]] + part[rel, out, mine, span[h]]
 
     def place(rel):
         rows = jnp.concatenate(lists(rel), axis=1)
@@ -214,14 +229,27 @@
 
         lax.fori_loop(0, n_rows // blk, body, 0)
 
-    def need(rel):
-        x_mate[rel].wait_recv()
-        d_mate[rel].wait_recv()
-
     n_wide = width // WIDE
     cut = width - LATE
-    for rel, flip in near_peers:
-        q_copies[rel, flip].wait_recv()
+    part_half = width // HALVES
+    early = [pl.ds(h * part_half, min(part_half, cut - h * part_half)) for h in range(HALVES)]
+
+    def send_near(rel, out, sends, target):
+        copies = []
+        for h in range(HALVES):
+            add_mate(rel, out, sends, h)
+            copies.append(rcopy(sib.at[rel, out, :, early[h]], near.at[out, :, early[h]], n_send.at[out, h], n_recv.at[out, h], target))
+            copies[-1].start()
+        return copies
+
+    def send_far(out, sends, target):
+        copies = []
+        for h in range(HALVES):
+            add_mate(FAR, out, sends, h)
+            copies.append(rcopy(sib.at[FAR, out, :, span[h]], far.at[out, :, span[h]], f_send.at[out, h], f_recv.at[out, h], target))
+            copies[-1].start()
+        return copies
+
     gather_hot((RIGHT, LEFT))
     load_u.wait()
     gather_rows((RIGHT, LEFT), u_v, ureq, 0, n_wide)
@@ -233,48 +261,64 @@
     d_mate[RIGHT].start()
     load_v.wait()
     gather_rows((RIGHT, LEFT), v_v, vreq, 0, n_wide)
-    for rel, flip in far_peers:
-        q_copies[rel, flip].wait_recv()
+    x_mate[LEFT].wait_recv()
+    dot_x(LEFT)
+    d_mate[RIGHT].wait_recv()
+    dot_d(RIGHT)
+    for copy in q_pass:
+        copy.wait_recv()
     gather_hot((FAR,))
-    gather_rows((FAR,), u_v, ureq, 0, 1)
     d_right.wait_recv()
     d_mate[LEFT].start()
     x_left.wait_recv()
     x_mate[RIGHT].start()
+    gather_rows((FAR,), u_v, ureq, 0, 1)
+    gates_here(LEFT)
+    coef(LEFT, 0)
+    s_left_y = partial(LEFT, 0)
+    gates_here(RIGHT)
+    x_mate[RIGHT].wait_recv()
+    dot_x(RIGHT)
+    coef(RIGHT, 1)
+    s_right_d = partial(RIGHT, 1)
+    for flip in range(2):
+        g_out[flip].wait_recv()
+        g_pass[flip].start()
+    n_left = send_near(LEFT, 0, s_left_y, left)
     gather_rows((FAR,), u_v, ureq, 1, n_wide)
-    need(RIGHT)
-    scores(RIGHT)
-    s_right_d = partial(RIGHT, 1)
-    need(LEFT)
-    scores(LEFT)
-    s_left_y = partial(LEFT, 0)
-    add_mate(RIGHT, 1, s_right_d)
-    n_right = rcopy(sib.at[RIGHT, 1, :, 0:cut], near.at[1], n_send.at[1], n_recv.at[1], right)
-    n_right.start()
-    add_mate(LEFT, 0, s_left_y)
-    n_left = rcopy(sib.at[LEFT, 0, :, 0:cut], near.at[0], n_send.at[0], n_recv.at[0], left)
-    n_left.start()
+    n_right = send_near(RIGHT, 1, s_right_d, right)
     gather_rows((FAR,), v_v, vreq, 0, n_wide)
     x_far.wait_recv()
     x_mate[FAR].start()
     d_far.wait_recv()
     d_mate[FAR].start()
+    d_mate[LEFT].wait_recv()
+    dot_d(LEFT)
+    coef(LEFT, 1)
+    coef(RIGHT, 0)
     s_right_y = partial(RIGHT, 0)
     s_left_d = partial(LEFT, 1)
-    need(FAR)
-    scores(FAR)
-    s_far = [partial(FAR, 0), partial(FAR, 1)]
-    add_mate(FAR, 0, s_far[0])
-    f_y = rcopy(sib.at[FAR, 0], far.at[0], f_send.at[0], f_recv.at[0], right)
-    f_y.start()
-    add_mate(FAR, 1, s_far[1])
-    f_d = rcopy(sib.at[FAR, 1], far.at[1], f_send.at[1], f_recv.at[1], left)
-    f_d.start()
+    gates_here(FAR)
+    x_mate[FAR].wait_recv()
+    dot_x(FAR)
+    coef(FAR, 0)
+    s_far_y = partial(FAR, 0)
+    d_mate[FAR].wait_recv()
+    dot_d(FAR)
+    coef(FAR, 1)
+    s_far_d = partial(FAR, 1)
+    f_y = send_far(0, s_far_y, right)
+    f_d = send_far(1, s_far_d, left)
     gather_hot((OWN,))
     gather_rows((OWN,), u_v, ureq, 0, n_wide)
     gather_rows((OWN,), v_v, vreq, 0, n_wide)
-    need(OWN)
-    scores(OWN)
+    x_mate[OWN].wait_recv()
+    d_mate[OWN].wait_recv()
+    gates_here(OWN)
+    dot_x(OWN)
+    dot_d(OWN)
+    coef(OWN, 0)
+    coef(OWN, 1)
     s_own = [partial(OWN, 0), partial(OWN, 1)]
     o_x = pltpu.make_async_copy(xa, xall_out, out_sem.at[0])
     o_d = pltpu.make_async_copy(da, dyall_out, out_sem.at[1])
@@ -286,39 +330,30 @@
     o_w = pltpu.make_async_copy(wt, wt_out, out_sem.at[3])
     o_c.start()
     o_w.start()
-    add_mate(RIGHT, 0, s_right_y)
-    add_mate(LEFT, 1, s_left_d)
-    add_mate(OWN, 0, s_own[0])
-    add_mate(OWN, 1, s_own[1])
-    n_left.wait_recv()
-    sib[OWN, 0, :, 0:cut] = sib[OWN, 0, :, 0:cut] + near[0]
-    n_right.wait_recv()
-    sib[OWN, 1, :, 0:cut] = sib[OWN, 1, :, 0:cut] + near[1]
-    o_own = pltpu.make_async_copy(sib.at[OWN], own_out, out_sem.at[4])
-    o_own.start()
-    o_rest = [pltpu.make_async_copy(sib.at[RIGHT, 1, :, cut:width], y_next.at[:, width:width + LATE], out_sem.at[7]),
-              pltpu.make_async_copy(sib.at[LEFT, 0, :, cut:width], dx_next.at[:, width:width + LATE], out_sem.at[8])]
-    for copy in o_rest:
-        copy.start()
-    for key in q_copies:
+    for h in range(HALVES):
+        add_mate(RIGHT, 0, s_right_y, h)
+        add_mate(LEFT, 1, s_left_d, h)
+        add_mate(OWN, 0, s_own[0], h)
+        add_mate(OWN, 1, s_own[1], h)
+    for h in range(HALVES):
+        for out, copies in enumerate((n_left, n_right)):
+            copies[h].wait_recv()
+            own_out[out, :, early[h]] = sib[OWN, out, :, early[h]] + near[out, :, early[h]]
+    own_out[:, :, cut:width] = sib[OWN, :, :, cut:width]
+    y_next[:, width:width + LATE] = sib[RIGHT, 1, :, cut:width]
+    dx_next[:, width:width + LATE] = sib[LEFT, 0, :, cut:width]
+    for h in range(HALVES):
+        for out, copies, rel, dst in ((0, f_y, RIGHT, y_next), (1, f_d, LEFT, dx_next)):
+            copies[h].wait_recv()
+            dst[:, span[h]] = sib[rel, out, :, span[h]] + far[out, :, span[h]]
+    for key in peers:
         q_copies[key].wait_send()
         g_copies[key].wait_send()
-    for copy in (x_right, d_left, d_right, x_left, x_far, d_far, *x_mate, *d_mate, *s_far, s_right_d, s_right_y, s_left_y, s_left_d, *s_own, n_left, n_right):
+    for copy in (*q_pass, *g_out, *g_pass, x_right, d_left, d_right, x_left, x_far, d_far, *x_mate, *d_mate, *s_far_y, *s_far_d, *s_right_d, *s_right_y, *s_left_y, *s_left_d,
+                 *s_own[0], *s_own[1], *n_left, *n_right, *f_y, *f_d):
         copy.wait_send()
-    for copy in (o_x, o_d, o_c, o_w, o_own, *o_rest):
+    for copy in (o_x, o_d, o_c, o_w):
         copy.wait()
-    f_y.wait_recv()
-    sib[RIGHT, 0] = sib[RIGHT, 0] + far[0]
-    o_y = pltpu.make_async_copy(sib.at[RIGHT, 0], y_next.at[:, 0:width], out_sem.at[5])
-    o_y.start()
-    f_d.wait_recv()
-    sib[LEFT, 1] = sib[LEFT, 1] + far[1]
-    o_dx = pltpu.make_async_copy(sib.at[LEFT, 1], dx_next.at[:, 0:width], out_sem.at[6])
-    o_dx.start()
-    f_y.wait_send()
-    f_d.wait_send()
-    o_y.wait()
-    o_dx.wait()
 
 
 def grad_kernel(ct_ref, wt_ref, xall_ref, dyall_ref, gu_ref, gv_ref):
@@ -333,6 +368,7 @@
     n_dev = mesh.shape['ep']
     tok_spec = P(('dp', 'ep'))
     table_spec = P('ep')
+    vmem = pl.BlockSpec(memory_space=pltpu.VMEM)
     hbm = pl.BlockSpec(memory_space=pl.ANY)
     dma = pltpu.SemaphoreType.DMA
     sds = jax.ShapeDtypeStruct
@@ -346,25 +382,25 @@
         y_next, dx_next, own, xall, dyall, ct, wt = pl.pallas_call(
             exchange_kernel,
             name='exchange',
-            out_shape=(sds((n_tok, width + LATE), F32), sds((n_tok, width + LATE), F32), sds((2, n_tok, width), F32),
+            out_shape=(pltpu.VMEM((n_tok, width + LATE), F32), pltpu.VMEM((n_tok, width + LATE), F32), pltpu.VMEM((2, n_tok, width), F32),
                        sds((4, 2, n_tok, width), BF16), sds((4, 2, n_tok, width), BF16), sds((n_rows, n_all), BF16), sds((n_rows, n_all), BF16)),
             in_specs=[hbm] * 7,
-            out_specs=(hbm,) * 7,
+            out_specs=(vmem,) * 3 + (hbm,) * 4,
             scratch_shapes=[
                 pltpu.VMEM((n_rows, width), BF16), pltpu.VMEM((n_rows, width), BF16),
                 pltpu.VMEM((n_dev * n_req, width), BF16), pltpu.VMEM((n_dev * n_req, width), BF16),
                 pltpu.VMEM((4 * n_req, n_rows), BF16),
                 pltpu.VMEM((4, 2, n_tok, width), BF16), pltpu.VMEM((4, 2, n_tok, width), BF16),
-                pltpu.VMEM((4, 2, n_tok, n_req), F32), pltpu.VMEM((4, 2, n_dev, n_req), jnp.int32),
+                pltpu.VMEM((4, 2, n_tok, n_req), F32), pltpu.VMEM((4, 2, n_dev, n_req), jnp.int32), pltpu.VMEM((2, n_tok, n_req), F32),
                 pltpu.VMEM((sel, n_tok), jnp.int32), pltpu.VMEM((sel, n_tok), F32), pltpu.VMEM((n_tok, sel), jnp.int32), pltpu.VMEM((n_tok, sel), F32),
                 pltpu.VMEM((n_tok * n_dev, n_req), F32), pltpu.VMEM((n_dev, n_tok, n_req), F32),
-                pltpu.VMEM((4, 4 * n_tok, 2 * n_req), BF16), pltpu.VMEM((n_rows, n_all), BF16), pltpu.VMEM((n_rows, n_all), BF16),
+                pltpu.VMEM((4, 2 * n_tok, 2 * n_req), F32), pltpu.VMEM((4, 2 * n_tok, 2 * n_req), F32), pltpu.VMEM((4, 4 * n_tok, 2 * n_req), BF16), pltpu.VMEM((n_rows, n_all), BF16), pltpu.VMEM((n_rows, n_all), BF16),
                 pltpu.VMEM((4, 2, 2 * n_tok, width), F32), pltpu.VMEM((4, 2, n_tok, width), F32),
                 pltpu.VMEM((2, n_tok, width - LATE), F32), pltpu.VMEM((2, n_tok, width), F32),
-                dma((7,)), dma((9,)), dma((7,)), dma((7,)), dma((7,)), dma((7,)), dma((6,)), dma((6,)), dma((4, 2)), dma((4, 2)),
-                dma((4, 2)), dma((4, 2)), dma((2,)), dma((2,)), dma((2,)), dma((2,)),
+                dma((7,)), dma((4,)), dma((7,)), dma((7,)), dma((9,)), dma((9,)), dma((6,)), dma((6,)), dma((4, 2)), dma((4, 2)),
+                dma((4, 2, HALVES)), dma((4, 2, HALVES)), dma((2, HALVES)), dma((2, HALVES)), dma((2, HALVES)), dma((2, HALVES)),
             ],
-            compiler_params=pltpu.CompilerParams(collective_id=0, has_side_effects=True, vmem_limit_bytes=60 * 2 ** 20),
+            compiler_params=pltpu.CompilerParams(collective_id=0, has_side_effects=True, vmem_limit_bytes=54 * 2 ** 20),
             cost_estimate=pl.CostEstimate(flops=4 * n_dev * n_req * n_rows * width, bytes_accessed=6 * n_rows * width, transcendentals=0),
         )(tokens, grad_out, slot_ids.reshape(n_tok, sel).T, gate_vals.reshape(n_tok, sel).T, request_rows[0], up_local, down_local)
 

time: 67.8 us -> 66.1 us (0.975)
  Pallas kernels: 63.4 us -> 60.9 us
    pallas_call x1, Pallas kernels: 49.8 us -> 47.4 us  [per_device(): pl.pallas_call(exchange_kernel, name='exchange', out_shape=(pltpu.VMEM((n...]
  transfers between devices with their start and end apart: 2 -> 2, of which waited for: 0 -> 1; matrix products, arithmetic and copies ran while one was open for 0% -> 0% of each run, Pallas kernels for 20% -> 21%
where the time goes in v3:
time: 66.1 us; the launch traced here: 65.8 us
  Pallas kernels  60.9 us (92%)
  starting transfers between devices  2.76 us (4%)
  other arithmetic  0.92 us (1%)
  between operations  0.67 us (1%)
    pallas_call x1, Pallas kernels, per_device(): pl.pallas_call(exchange_kernel, name='exchange', out_shape=(pltpu.VMEM((n...  47.4 us
    pallas_call x1, Pallas kernels, per_device(): pl.pallas_call(grad_kernel, name='table_grads', out_shape=(sds((n_rows, w...  13.5 us
    ppermute x1, starting transfers between devices, per_device(): dx_last = lax.ppermute(dx_next, 'ep', down_chip)  2.65 us
  transfers between devices with their start and end apart: 2, of which 1 were waited for; matrix products, arithmetic and copies ran while one was open for 0% of the time, Pallas kernels for 21%

profile of v3, /device:TPU:81, one launch (start us, length us, event | category | flops | bytes accessed | tf_op | source)
XLA Modules:
  0.0 65.8 jit_solution(5667672399401456744)
XLA Ops:
  0.6 47.4 %exchange.1 = (f32[64,2560]{1,0:T(8,128)S(1)}, f32[64,2560]{1,0:T(8,128)S(1)}, f32[2,64,2048]{2,1,0:T(8,128)S(1)}, bf16[4,2,64,2048]{3,2,1,0:T(8,128)(2,1)}, bf1...) custom-call(bf16[64,2048]{1,0:T(8,128)(2,1)} %x_hbm.1, ...), custom_call_target="tpu_custom_call" | custom-call | flops 17179869184 | bytes 25165824 | tf_op jit(solution)/shard_map/exchange/pallas_call | solution.py:382
  48.0 0.1 collective-permute-start
  48.1 2.6 %collective-permute-start.1 = (f32[64,2560]{1,0:T(8,128)S(1)}, f32[64,2560]{1,0:T(8,128)S(1)}, u32[]{:S(2)}, u32[]{:S(2)}) collective-permute-start(f32[64,2560]{1,0:T(8,128)S(1)} %get-tuple-element.15), channel_id=1, source_target_pairs={{0,6},{1,7},{2,0},{3,1},{4,2},{5,3},{6,4},{7,5},{8,14},{9,15},{10,... | collective-permute-start | bytes 1966088 | tf_op jit(solution)/shard_map/ppermute | solution.py:410
  50.8 13.5 %table_grads.1 = (bf16[2048,2048]{1,0:T(8,128)(2,1)}, bf16[2048,2048]{1,0:T(8,128)(2,1)}) custom-call(bf16[2048,512]{1,0:T(8,128)(2,1)} %get-tuple-element.16.ct_ref, bf16[2048,512]{1,0:T(8,128)(2,1)} %get-tuple-element.17.wt_ref, bf16[512,2048]{1,0:T(8,128)(2,1)} %bitcast.16, bf16[512,2048]{1,0:T(8,128)(2,1)} %bitcast.17), custom_call_target="tpu_custom_call" | custom-call | flops 8589934592 | bytes 20971520 | tf_op jit(solution)/shard_map/table_grads/pallas_call | solution.py:415
  64.3 0.6 collective-permute-done
  64.9 0.0 collective-permute-done.1
  64.9 0.9 %fusion.1 = (bf16[64,2048]{1,0:T(8,128)(2,1)}, bf16[64,2048]{1,0:T(8,128)(2,1)}) fusion(f32[64,2560]{1,0:T(8,128)S(1)} %collective-permute-done.1, f32[64,512]{1,0:T(8,128)S(1)} %slice.27, f32[2,64,2048]{2,1,0:T(8,128)S(1)} %get-tuple-element.13, f32[64,512]{1,0:T(8,128)S(1)} %slice.25, f32[64,2560]{1,0:T(8,128)S(1)} %collective-permute-done), kind=kLoop, calls=%fused_computation.2 | loop fusion | flops 786432 | bytes 2883584 | tf_op jit(solution)/shard_map/convert_element_type | solution.py:428
  (2 shorter events, 0.0 us)
Async XLA Ops:
  48.0 16.8 %collective-permute-start = (f32[64,2560]{1,0:T(8,128)S(1)}, f32[64,2560]{1,0:T(8,128)S(1)}, u32[]{:S(2)}, u32[]{:S(2)}) collective-permute-start(f32[64,2560]{1,0:T(8,128)S(1)} %get-tuple-element.14), channel_id=1, source_target_pairs={{0,2},{1,3},{2,4},{3,5},{4,6},{5,7},{6,0},{7,1},{8,10},{9,11},{10,... | collective-permute-start | bytes 1966088 | tf_op jit(solution)/shard_map/ppermute | solution.py:409
  48.1 16.7 %collective-permute-start.1 = (f32[64,2560]{1,0:T(8,128)S(1)}, f32[64,2560]{1,0:T(8,128)S(1)}, u32[]{:S(2)}, u32[]{:S(2)}) collective-permute-start(f32[64,2560]{1,0:T(8,128)S(1)} %get-tuple-element.15), channel_id=1, source_target_pairs={{0,6},{1,7},{2,0},{3,1},{4,2},{5,3},{6,4},{7,5},{8,14},{9,15},{10,... | collective-permute-start | bytes 1966088 | tf_op jit(solution)/shard_map/ppermute | solution.py:410

commit v4 on v3

--- a/solution.py
+++ b/solution.py
@@ -17,7 +17,7 @@
 COLS = 512
 WIDE = 1024
 LATE = 512
-HALVES = 2
+HALVES = 1
 
 
 def gelu_pair(pre_act):

time: 66.1 us -> 66.1 us (level)
  no operation moved by 1% of the time
where the time goes in v4:
time: 66.1 us; the launch traced here: 65.9 us
  Pallas kernels  60.9 us (92%)
  starting transfers between devices  2.76 us (4%)
  other arithmetic  0.92 us (1%)
  between operations  0.67 us (1%)
    pallas_call x1, Pallas kernels, per_device(): pl.pallas_call(exchange_kernel, name='exchange', out_shape=(pltpu.VMEM((n...  47.4 us
    pallas_call x1, Pallas kernels, per_device(): pl.pallas_call(grad_kernel, name='table_grads', out_shape=(sds((n_rows, w...  13.5 us
    ppermute x1, starting transfers between devices, per_device(): dx_last = lax.ppermute(dx_next, 'ep', down_chip)  2.65 us
  transfers between devices with their start and end apart: 2, of which 1 were waited for; matrix products, arithmetic and copies ran while one was open for 0% of the time, Pallas kernels for 21%

profile of v4, /device:TPU:81, one launch (start us, length us, event | category | flops | bytes accessed | tf_op | source)
XLA Modules:
  0.0 65.9 jit_solution(7105663043268377549)
XLA Ops:
  0.6 47.4 %exchange.1 = (f32[64,2560]{1,0:T(8,128)S(1)}, f32[64,2560]{1,0:T(8,128)S(1)}, f32[2,64,2048]{2,1,0:T(8,128)S(1)}, bf16[4,2,64,2048]{3,2,1,0:T(8,128)(2,1)}, bf1...) custom-call(bf16[64,2048]{1,0:T(8,128)(2,1)} %x_hbm.1, ...), custom_call_target="tpu_custom_call" | custom-call | flops 17179869184 | bytes 25165824 | tf_op jit(solution)/shard_map/exchange/pallas_call | solution.py:382
  48.0 0.1 collective-permute-start
  48.1 2.6 %collective-permute-start.1 = (f32[64,2560]{1,0:T(8,128)S(1)}, f32[64,2560]{1,0:T(8,128)S(1)}, u32[]{:S(2)}, u32[]{:S(2)}) collective-permute-start(f32[64,2560]{1,0:T(8,128)S(1)} %get-tuple-element.15), channel_id=1, source_target_pairs={{0,6},{1,7},{2,0},{3,1},{4,2},{5,3},{6,4},{7,5},{8,14},{9,15},{10,... | collective-permute-start | bytes 1966088 | tf_op jit(solution)/shard_map/ppermute | solution.py:410
  50.8 13.5 %table_grads.1 = (bf16[2048,2048]{1,0:T(8,128)(2,1)}, bf16[2048,2048]{1,0:T(8,128)(2,1)}) custom-call(bf16[2048,512]{1,0:T(8,128)(2,1)} %get-tuple-element.16.ct_ref, bf16[2048,512]{1,0:T(8,128)(2,1)} %get-tuple-element.17.wt_ref, bf16[512,2048]{1,0:T(8,128)(2,1)} %bitcast.16, bf16[512,2048]{1,0:T(8,128)(2,1)} %bitcast.17), custom_call_target="tpu_custom_call" | custom-call | flops 8589934592 | bytes 20971520 | tf_op jit(solution)/shard_map/table_grads/pallas_call | solution.py:415
  64.3 0.6 collective-permute-done
  65.0 0.0 collective-permute-done.1
  65.0 0.9 %fusion.1 = (bf16[64,2048]{1,0:T(8,128)(2,1)}, bf16[64,2048]{1,0:T(8,128)(2,1)}) fusion(f32[64,2560]{1,0:T(8,128)S(1)} %collective-permute-done.1, f32[64,512]{1,0:T(8,128)S(1)} %slice.27, f32[2,64,2048]{2,1,0:T(8,128)S(1)} %get-tuple-element.13, f32[64,512]{1,0:T(8,128)S(1)} %slice.25, f32[64,2560]{1,0:T(8,128)S(1)} %collective-permute-done), kind=kLoop, calls=%fused_computation.2 | loop fusion | flops 786432 | bytes 2883584 | tf_op jit(solution)/shard_map/convert_element_type | solution.py:428
  (2 shorter events, 0.0 us)
Async XLA Ops:
  48.0 16.9 %collective-permute-start = (f32[64,2560]{1,0:T(8,128)S(1)}, f32[64,2560]{1,0:T(8,128)S(1)}, u32[]{:S(2)}, u32[]{:S(2)}) collective-permute-start(f32[64,2560]{1,0:T(8,128)S(1)} %get-tuple-element.14), channel_id=1, source_target_pairs={{0,2},{1,3},{2,4},{3,5},{4,6},{5,7},{6,0},{7,1},{8,10},{9,11},{10,... | collective-permute-start | bytes 1966088 | tf_op jit(solution)/shard_map/ppermute | solution.py:409
  48.1 16.8 %collective-permute-start.1 = (f32[64,2560]{1,0:T(8,128)S(1)}, f32[64,2560]{1,0:T(8,128)S(1)}, u32[]{:S(2)}, u32[]{:S(2)}) collective-permute-start(f32[64,2560]{1,0:T(8,128)S(1)} %get-tuple-element.15), channel_id=1, source_target_pairs={{0,6},{1,7},{2,0},{3,1},{4,2},{5,3},{6,4},{7,5},{8,14},{9,15},{10,... | collective-permute-start | bytes 1966088 | tf_op jit(solution)/shard_map/ppermute | solution.py:410
